TPU v7x, 128 devices: a whole 4x4x4 slice. The times are simulated.
128 devices in a mesh: row: 8 (over z, core), col: 16 (over y, x).
Axes of the slice: x: 4, y: 4, z: 4, core: 2. Of those that a mesh axis runs over, the one named last changes fastest.
Arguments:
- load_amp: float32 [4096, 8192], P('row', 'col'), may hold values from 0.05 to 1
- load_mask: int32 [4096, 8192], P('row', 'col'), may hold values 0 or 1
- leak: float32 [4096, 8192], P('row', 'col'), may hold values from 0.001 to 0.05
- coarse_leak: float32 [1024, 2048], P('row', 'col'), may hold values from 0.01 to 0.5
- coarse_init: float32 [1024, 2048], P('row', 'col'), may hold values from 0 to 1
- via_fine: int32 [8, 32768], P('row', 'col'), may hold values from 0 to 262143
- via_coarse: int32 [8, 32768], P('row', 'col'), may hold values from 0 to 262143, as said below
- via_count: int32 [8, 256], P('row', 'col'), may hold values from 0 to 128, as said below
Outputs:
- fine_drop: float32 [4096, 8192], P('row', 'col')
- coarse_drop: float32 [1024, 2048], P('row', 'col')
Inputs may be any that keep to these rules, and one draw needn't show every extreme that they name: `via_coarse`: slot s of a tile names a coarse node whose stored column lies in s // 128 * 128 to s // 128 * 128 + 127. `via_count`: slots of an owner past its count are padding and carry arbitrary indices. In each tile row some owner gets 128 live slots from every tile of that row.
All inputs are finite; a program needn't handle non-finite values. No bound on the sum of `load_mask` on one device may be relied on, other than what follows from the above.
Results may differ from a plain program's by a relative error of at most 0.00022.
Values sent between devices are 32-bit elements; how exact they have to be, the bound alone decides.
No kernel may reach another device: no remote copies, remote signals or barrier semaphores. Data moves between devices by JAX's collectives and lax.ppermute only.
A program may use at most 64 MiB of HBM per device.

v0:
```python
import jax
import jax.numpy as jnp
from jax import lax
from jax.experimental import pallas as pl
from jax.experimental.pallas import tpu as pltpu
from jax.sharding import PartitionSpec as P


F32 = jnp.float32
BF16 = jnp.bfloat16
HI = lax.Precision.HIGHEST
ROW, COL = "row", "col"

GROUP = 16
via_conductance = 2.0
coarse_conductance = 4.0
relaxation = 0.8

T = 512
CB = 128
NO = 16
L = 128
OFF = 16
EXT = OFF + T + 16
W = T + L

Q = (1.09375, 1.765625, 1.28125)
RHO = (1.0 - Q[0], Q[0] - Q[1], Q[1] - Q[2], Q[2])
LT = T // L
SLAB = 4 * LT + 1
SUMS = 8
AHEAD = 1
STEPS = 8


def iota(shape, dim):
    return lax.broadcasted_iota(jnp.int32, shape, dim)


def nt(a, b, precision=None):
    return lax.dot_general(
        a, b, (((1,), (1,)), ((), ())), precision=precision, preferred_element_type=F32
    )


def tn(a, b, precision=None):
    return lax.dot_general(
        a, b, (((0,), (0,)), ((), ())), precision=precision, preferred_element_type=F32
    )


def onehot(idx, n):
    return jnp.where(iota((n, idx.shape[1]), 0) == idx, 1.0, 0.0).astype(BF16)


def hi_lo(x):
    hi = x.astype(BF16).astype(F32)
    return hi, x - hi


def lanes(o):
    return slice(o * L, (o + 1) * L)


def at(pos, k, like):
    return jnp.broadcast_to(pos[k : k + 1, : like.shape[1]], like.shape)


def pair_order(pos, k, low, high):
    even = (at(pos, k, low) & 1) == 0
    return jnp.where(even, high, low), jnp.where(even, low, high)


def from_pairs(pos, k, first, second):
    even = (at(pos, k, first) & 1) == 0
    return jnp.where(even, second, first), jnp.where(even, first, second)


def diag_kernel(
    amp, mask, leak, via, zl, invd, strips, rims, amp_s, mask_s, leak_s, via_s, sem
):
    copies = [
        pltpu.make_async_copy(x, y, sem.at[k])
        for k, (x, y) in enumerate(
            ((leak, leak_s), (via, via_s), (amp, amp_s), (mask, mask_s))
        )
    ]
    for copy in copies:
        copy.start()
    for copy in copies:
        copy.wait()
    inv = 1.0 / (4.0 + leak_s[...] + via_s[...])
    z = amp_s[...] * mask_s[...].astype(F32) * inv
    zl[...] = z
    invd[...] = inv
    j, lane = iota((8, 2 * L), 0), iota((8, 2 * L), 1)
    pick = jnp.where(lane == jnp.where(j < 4, j, 2 * L - 8 + j), 1.0, 0.0).astype(BF16)
    for k, x in enumerate((z, inv)):
        hi, rest = hi_lo(jnp.concatenate([x[:, :L], x[:, T - L :]], axis=1))
        mid, lo = hi_lo(rest)
        strips[8 * k : 8 * k + 8, :] = (
            nt(pick, lo.astype(BF16)) + nt(pick, mid.astype(BF16)) + nt(pick, hi.astype(BF16))
        )
    rims[0:8, :] = inv[0:8]
    rims[8:16, :] = inv[T - 8 :]


def copies_kernel(volt, out, sem):
    copies = [
        pltpu.make_async_copy(volt, out.at[pl.ds(o * CB, CB), :], sem.at[o]) for o in range(NO)
    ]
    for copy in copies:
        copy.start()
    for copy in copies:
        copy.wait()


def parts_kernel(vf, vc, wt, node, slots, vf_o, via, a_s, b_s):
    f = vf[...]
    vf_o[...] = f
    slots[0:NO, :] = (f >> 9) * SLAB + ((f >> 7) & 3) * 4
    slots[NO:, :] = (iota((NO, L), 1) - f) & (L - 1)
    place = ((vc[...] >> 11) << 7) | (vc[...] & (CB - 1))
    node[...] = jnp.where(wt[...] > 0.0, place.astype(F32), -1.0)
    for o in range(NO):
        f = vf[o : o + 1, :]
        a_s[:, lanes(o)] = onehot(f // T, T)
        b_s[:, lanes(o)] = jnp.where(iota((T, L), 0) == f % T, wt[o : o + 1, :], 0.0).astype(BF16)
    via[...] = nt(a_s[...], b_s[...])


def strips_kernel(pos, blocks, node, vf, wt, strips, a_o, send_1, send_2, inj_o):
    for o in range(NO):
        at_node = node[o : o + 1, :].astype(jnp.int32)
        v1, rest = hi_lo(blocks[o * CB : (o + 1) * CB, :])
        v2, v3 = hi_lo(rest)
        v = jnp.concatenate([v3, v2, v1], axis=0).astype(BF16)
        y = jnp.dot(v, onehot(at_node & (CB - 1), CB), preferred_element_type=F32)
        y = y[:CB] + y[CB : 2 * CB] + y[2 * CB :]
        y = jnp.where(iota((CB, L), 0) == (at_node >> 7), y, 0.0)
        inj_o[o : o + 1, :] = jnp.sum(y, axis=0, keepdims=True) * wt[o : o + 1, :]
    j = iota((8, L), 0)
    colid = jnp.where(j < 4, j, T - 8 + j)
    hs, ls = [], []
    for o in range(NO):
        f = vf[o : o + 1, :]
        a_o[:, lanes(o)] = onehot(f // T, T)
        hi, lo = hi_lo(inj_o[o : o + 1, :])
        on = colid == f % T
        hs.append(jnp.where(on, hi, 0.0))
        ls.append(jnp.where(on, lo, 0.0))
    lhs = jnp.concatenate(
        [jnp.concatenate(hs, axis=1), jnp.concatenate(ls, axis=1)], axis=0
    ).astype(BF16)
    inj = nt(lhs, a_o[...])
    inv = strips[8:16, :]
    z = strips[0:8, :] + (inj[0:8] + inj[8:16]) * inv
    low = iota((8, T), 0) < 4
    to_l = jnp.where(low, z, pltpu.roll(inv, 4, 0))
    to_r = jnp.where(low, pltpu.roll(z, 4, 0), inv)
    send_1[...], send_2[...] = pair_order(pos, 1, to_l, to_r)


def rhs_kernel(vf, injected, zl, invd, a, z, rims, b_s):
    for o in range(NO):
        hi, lo = hi_lo(injected[o : o + 1, :])
        on = iota((T, L), 0) == vf[o : o + 1, :] % T
        b_s[:, lanes(o)] = jnp.where(on, hi, 0.0).astype(BF16)
        b_s[:, lanes(NO + o)] = jnp.where(on, lo, 0.0).astype(BF16)
    inj = nt(a[...], b_s[:, : NO * L]) + nt(a[...], b_s[:, NO * L :])
    zz = zl[...] + inj * invd[...]
    z[...] = zz
    rims[0:8, :] = zz[0:8]
    rims[8:16, :] = zz[T - 8 :]


def halo_columns(pos, gl, gr):
    place = at(pos, 1, gl)
    parts = []
    for x in (jnp.where(place < NO - 1, gr, 0.0), jnp.where(place > 0, gl, 0.0)):
        a, rest = hi_lo(x)
        b, c = hi_lo(rest)
        parts += [c, b, a]
    j, lane = iota((8, 2 * L), 0), iota((8, 2 * L), 1)
    to_r = jnp.where(lane == jnp.where(j < 4, j, L + j - 4), 1.0, 0.0)
    to_l = jnp.where(lane == jnp.where(j < 4, 124 + j, L + 120 + j), 1.0, 0.0)
    place = jnp.concatenate([to_r] * 3 + [to_l] * 3, axis=0)
    out = tn(jnp.concatenate(parts, axis=0).astype(BF16), place.astype(BF16))
    return out[:, :L], out[:, L:]


def edge_kernel(pos, zr, ir, col_1, col_2, volt, send_1, send_2, corners):
    got_l, got_r = from_pairs(pos, 1, col_1[...], col_2[...])
    zt, it = halo_columns(pos, got_l[:, :L], got_r[:, :L])
    zb, ib = halo_columns(pos, got_l[:, T - L : T], got_r[:, T - L : T])
    for k, x in enumerate((zt[0:16], zb[L - 16 :], it[0:16], ib[L - 16 :])):
        corners[16 * k : 16 * k + 16, :] = x
    low = iota((8, W), 0) < 4
    zt = jnp.concatenate([zr[0:8, :], zt[0:8]], axis=1)
    it = jnp.concatenate([ir[0:8, :], it[0:8]], axis=1)
    zb = jnp.concatenate([zr[8:16, :], zb[L - 8 :]], axis=1)
    ib = jnp.concatenate([ir[8:16, :], ib[L - 8 :]], axis=1)
    to_u = jnp.where(low, zt, pltpu.roll(it, 4, 0))
    to_d = jnp.where(low, pltpu.roll(zb, 4, 0), ib)
    send_1[:, :W], send_2[:, :W] = pair_order(pos, 0, to_u, to_d)
    send_1[:, W:], send_2[:, W:] = pair_order(pos, 0, volt[0:8, :], volt[CB - 8 :, :])


def beside(block):
    n = block.shape[0]
    rows = pltpu.roll(block, 1, 0) + pltpu.roll(block, n - 1, 0)
    return rows + (pltpu.roll(block, 1, 1) + pltpu.roll(block, W - 1, 1))


def near_tiles(ref, start, rows):
    mid = [ref[t, pl.ds(start, rows), :] for t in range(LT + 1)]
    low = [pltpu.roll(m, 1, 1) for m in mid]
    high = [pltpu.roll(m, L - 1, 1) for m in mid]
    lane = iota((rows, L), 1)
    near = []
    for t in range(LT + 1):
        rows_sum = ref[t, pl.ds(start - 1, rows), :] + ref[t, pl.ds(start + 1, rows), :]
        left = jnp.where(lane == 0, low[t - 1], low[t])
        right = jnp.where(lane == L - 1, high[(t + 1) % (LT + 1)], high[t])
        near.append(rows_sum + (left + right))
    return mid, near


def fold(p):
    return (p[:, 0:128] + p[:, 128:256]) + (p[:, 256:384] + p[:, 384:512])


def moments(z, w, n1, n2, dn3, inv):
    d = 1.0 / inv
    dz, dw, dn1, dn2 = d * z, d * w, d * n1, d * n2
    return dz * z, dz * w, dw * w, dw * n1, dn1 * n1, dn1 * n2, dn2 * n2, n2 * dn3


def basis_kernel(pos, z, invd, col_1, col_2, hist, acc_o, ie, ze, we, n1e, n2e, sem):
    zc, ic = halo_columns(pos, *from_pairs(pos, 1, col_1[:, :T], col_2[:, :T]))
    zero = jnp.zeros((OFF, L), F32)
    own = pl.ds(OFF, T)
    for e in (ie, ze, we, n1e, n2e):
        for t in range(LT + 1):
            e[t, 0:OFF, :] = zero
            e[t, OFF + T :, :] = zero
    for t in range(LT):
        ze[t, own, :] = z[:, lanes(t)]
        ie[t, own, :] = invd[:, lanes(t)]
    ze[LT, own, :] = zc
    ie[LT, own, :] = ic
    rows = 128

    def save(k, e):
        copy = pltpu.make_async_copy(e.at[pl.ds(0, LT), own, :], hist.at[k], sem.at[k])
        copy.start()
        return copy

    def apply_to(src, dst, minus):
        def step(i, carry):
            start = pl.multiple_of(OFF + i * rows, 8)
            mid, near = near_tiles(src, start, rows)
            for t in range(LT + 1):
                y = near[t] * ie[t, pl.ds(start, rows), :]
                dst[t, pl.ds(start, rows), :] = mid[t] - y if minus else y
            return carry

        lax.fori_loop(0, T // rows, step, 0)

    copies = [save(0, ze)]
    apply_to(ze, we, True)
    copies.append(save(1, we))
    apply_to(we, n1e, False)
    copies.append(save(2, n1e))
    apply_to(n1e, n2e, False)
    copies.append(save(3, n2e))

    acc = [jnp.zeros((8, L), F32) for _ in range(SUMS)]
    ends = list(range(0, T + 1, 64))
    ends[0], ends[-1] = 8, T - 8
    for low, high in zip(ends[:-1], ends[1:]):
        start, rows = OFF + low, high - low
        n2, dn3 = near_tiles(n2e, start, rows)
        for t in range(LT):
            z8, w8, n18, i8 = (e[t, pl.ds(start, rows), :] for e in (ze, we, n1e, ie))
            for k, p in enumerate(moments(z8, w8, n18, n2[t], dn3[t], i8)):
                for q in range(0, rows, 8):
                    acc[k] = acc[k] + p[q : q + 8]
    for k in range(SUMS):
        acc_o[8 * k : 8 * k + 8, :] = acc[k]
    for copy in copies:
        copy.wait()


def gram_terms(acc):
    g0, q0 = acc[0], acc[1]
    m = acc[2:]
    r = [q0, q0 - m[0], q0 - m[0] - m[1]]
    h = {(0, 0): q0, **{(0, j): RHO[0] * m[j - 1] for j in (1, 2, 3)}}
    b = [g0] + r
    for k in range(3):
        h[0, 0] = h[0, 0] - Q[k] * m[k]
        b[0] = b[0] - Q[k] * r[k]
    for k in range(6):
        f = sum(Q[j] * RHO[k - j] for j in range(3) if 0 <= k - j < 4)
        h[0, 0] = h[0, 0] - f * m[k]
    for j in (1, 2, 3):
        for k in (1, 2, 3):
            h[0, j] = h[0, j] + RHO[k] * m[j - 1 + k]
            if j <= k:
                h[j, k] = m[j + k - 2] - m[j + k - 1]
    out = []
    for p in range(4):
        out += [h[p, q] for q in range(p, 4)] + [b[p]]
    return out


def rim_kernel(pos, z, invd, corners, row_1, row_2, acc_i, rims, part):
    sub = iota((8, W), 0)
    ours = at(pos, 0, sub)
    above, below = (sub >= 4) & (ours > 0), (sub < 4) & (ours < 7)
    top, bot = from_pairs(pos, 0, row_1[:, :W], row_2[:, :W])
    acc = [acc_i[8 * k : 8 * k + 8, :] for k in range(SUMS)]
    for end in (0, 1):
        rows = slice(0, 16) if end == 0 else slice(T - 16, T)
        zc, ic = corners[16 * end : 16 * end + 16, :], corners[32 + 16 * end : 48 + 16 * end, :]
        z16 = jnp.concatenate([z[rows, :], zc], axis=1)
        i16 = jnp.concatenate([invd[rows, :], ic], axis=1)
        if end == 0:
            zb = jnp.concatenate([jnp.where(above, pltpu.roll(top, 4, 0), 0.0), z16], axis=0)
            ib = jnp.concatenate([jnp.where(above, top, 0.0), i16], axis=0)
            own = slice(8, 16)
        else:
            zb = jnp.concatenate([z16, jnp.where(below, bot, 0.0)], axis=0)
            ib = jnp.concatenate([i16, jnp.where(below, pltpu.roll(bot, 4, 0), 0.0)], axis=0)
            own = slice(8, 16)
        w = zb - ib * beside(zb)
        n1 = ib * beside(w)
        n2 = ib * beside(n1)
        near = beside(n2)
        zo, wo, n1o, n2o, dn3, io = (x[own, :T] for x in (zb, w, n1, n2, near, ib))
        for k, p in enumerate(moments(zo, wo, n1o, n2o, dn3, io)):
            acc[k] = acc[k] + fold(p)
        for k, x in enumerate((wo, n1o, n2o)):
            rims[16 * k + 8 * end : 16 * k + 8 * end + 8, :] = x
    terms = gram_terms(acc)
    rows14 = jnp.concatenate(
        [jnp.sum(a, axis=0, keepdims=True) for a in terms] + [jnp.zeros((2, L), F32)], axis=0
    )
    a, rest = hi_lo(rows14)
    b, c = hi_lo(rest)
    parts = jnp.concatenate([c, b, a], axis=0).astype(BF16)
    sums = nt(jnp.ones((8, L), BF16), parts)
    sums = sums[:, 0:16] + sums[:, 16:32] + sums[:, 32:48]
    sums = jnp.concatenate([sums, jnp.zeros((8, L - 16), F32)], axis=1)
    part[...] = sums


def gather_kernel(hist, table, rims, wt, g_o, x_s, slab, slots, sem):
    copies = [pltpu.make_async_copy(hist.at[k], x_s.at[k], sem.at[k]) for k in range(4)]
    ready = pltpu.make_async_copy(table, slots, sem.at[4])
    ready.start()
    for copy in copies:
        copy.start()
    for k in range(4):
        copies[k].wait()
        if k:
            for t in range(LT):
                x_s[k, t, 0:8, :] = rims[16 * k - 16 : 16 * k - 8, lanes(t)]
                x_s[k, t, T - 8 :, :] = rims[16 * k - 8 : 16 * k, lanes(t)]

        def lay(i, carry):
            for b in range(4):
                for t in range(LT):
                    start = pl.multiple_of(i * 32 + 8 * b, 8)
                    to = (i * 32 + 8 * b) * SLAB + 4 * t + k
                    slab[pl.ds(to, 8, stride=SLAB), :] = x_s[k, t, pl.ds(start, 8), :]
            return carry

        lax.fori_loop(0, T // 32, lay, 0)
    lane, sub = iota((8, L), 1), iota((8, L), 0)
    ready.wait()
    for o in range(NO):
        acc = jnp.zeros((8, L), F32)
        for j in range(L):
            x = slab[pl.ds(slots[o, j], 8), :]
            acc = jnp.where(lane == j, pltpu.roll(x, slots[NO + o, j], 1), acc)
        g_o[8 * o : 8 * o + 8, :] = jnp.where(sub < 4, acc * wt[o : o + 1, :], 0.0)


def pack_kernel(g, rows, node, out):
    out[...] = g[...]
    total = jnp.sum(rows[...], axis=0, keepdims=True)
    for o in range(NO):
        out[8 * o + 4 : 8 * o + 5, :] = total
        out[8 * o + 5 : 8 * o + 6, :] = node[o : o + 1, :]


def solve(tot):
    lane = iota((1, L), 1)

    def pick(k):
        return jnp.sum(jnp.where(lane == k, tot, 0.0), axis=1, keepdims=True)

    h, b = {}, []
    k = 0
    for p in range(4):
        for q in range(p, 4):
            h[p, q] = pick(k)
            k += 1
        b.append(pick(k))
        k += 1
    floor = [3e-7 * h[p, p] for p in range(4)]
    inv = []
    for p in range(4):
        inv.append(jnp.where(h[p, p] > floor[p], 1.0 / h[p, p], 0.0))
        for q in range(p + 1, 4):
            f = h[p, q] * inv[p]
            for r in range(q, 4):
                h[q, r] = h[q, r] - f * h[p, r]
            b[q] = b[q] - f * b[p]
    c = [None] * 4
    for p in (3, 2, 1, 0):
        s = b[p]
        for q in range(p + 1, 4):
            s = s - h[p, q] * c[q]
        c[p] = s * inv[p]
    return [c[0]] + [c[k + 1] - Q[k] * c[0] for k in range(3)]


def combine_kernel(hist, ahead, coef, rims, out, h_s, x_s, sem_in, sem_out):
    n = T // STEPS
    load = [
        pltpu.make_async_copy(
            hist.at[pl.ds(AHEAD, 4 - AHEAD), :, pl.ds(i * n, n), :], h_s.at[i], sem_in.at[i]
        )
        for i in range(STEPS)
    ]
    save = [
        pltpu.make_async_copy(x_s.at[pl.ds(i * n, n), :], out.at[pl.ds(i * n, n), :], sem_out.at[i])
        for i in range(STEPS)
    ]
    for copy in load:
        copy.start()
    c = [coef[k : k + 1, 0:1] for k in range(4)]
    for i in range(STEPS):
        load[i].wait()
        for t in range(LT):
            h = [ahead[k, t, i * n : (i + 1) * n, :] for k in range(AHEAD)]
            h += [h_s[i, k, t] for k in range(4 - AHEAD)]
            x_s[i * n : (i + 1) * n, lanes(t)] = (c[0] * h[0] + c[1] * h[1]) + (
                c[2] * h[2] + c[3] * h[3]
            )
        for end, step, low in ((0, 0, 0), (1, STEPS - 1, n - 8)):
            if i == step:
                for t in range(LT):
                    x = c[0] * ahead[0, t, i * n + low : i * n + low + 8, :]
                    for k in range(3):
                        x += c[k + 1] * rims[16 * k + 8 * end : 16 * k + 8 * end + 8, lanes(t)]
                    x_s[i * n + low : i * n + low + 8, lanes(t)] = x
        save[i].start()
    for copy in save:
        copy.wait()


def coarse_neighbours(pos, u, row_1, row_2, from_l, from_r):
    above, below = from_pairs(pos, 0, row_1, row_2)
    above, below = above[7:8, :], below[0:1, :]
    above = jnp.where(at(pos, 0, above) > 0, above, 0.0)
    below = jnp.where(at(pos, 0, below) < 7, below, 0.0)
    r, lane = iota((CB, CB), 0), iota((CB, CB), 1)
    g, gl = iota((8, CB), 0), iota((8, CB), 1)
    turned_l = jnp.where(g == 0, 0.0, pltpu.roll(from_l, 1, 0))
    turned_r = jnp.where(g == 7, 0.0, pltpu.roll(from_r, 7, 0))
    place = at(pos, 1, from_l)
    from_l = jnp.where(place == 0, turned_l, from_l)
    from_r = jnp.where(place == NO - 1, turned_r, from_r)
    seam_l = tn(from_l, jnp.where(gl == g * GROUP, 1.0, 0.0), HI)
    seam_r = tn(from_r, jnp.where(gl == g * GROUP + GROUP - 1, 1.0, 0.0), HI)
    near = jnp.where(r == 0, above, pltpu.roll(u, 1, 0))
    near += jnp.where(r == CB - 1, below, pltpu.roll(u, CB - 1, 0))
    near += jnp.where(lane % GROUP == 0, seam_l, pltpu.roll(u, 1, 1))
    near += jnp.where(lane % GROUP == GROUP - 1, seam_r, pltpu.roll(u, CB - 1, 1))
    return near


def sweep(u, src, diag, near):
    return u + relaxation * (src - (diag * u - coarse_conductance * near)) / diag


def base_kernel(hist, blocks, pos, volt, row_1, row_2, near, ahead, b_s, sem):
    copy = pltpu.make_async_copy(hist.at[pl.ds(0, AHEAD)], ahead, sem.at[0])
    drops = pltpu.make_async_copy(blocks, b_s, sem.at[1])
    drops.start()
    copy.start()
    drops.wait()
    left, right = jnp.zeros((CB, CB), F32), jnp.zeros((CB, CB), F32)
    for o in range(NO):
        block = b_s[o * CB : (o + 1) * CB, :]
        ours = at(pos, 1, block)
        left = jnp.where(ours == (o + 1) % NO, block, left)
        right = jnp.where(ours == (o - 1) % NO, block, right)
    g, lane = iota((8, CB), 0), iota((8, CB), 1)
    from_l = nt(jnp.where(lane == g * GROUP + GROUP - 1, 1.0, 0.0), left, HI)
    from_r = nt(jnp.where(lane == g * GROUP, 1.0, 0.0), right, HI)
    near[...] = coarse_neighbours(pos, volt[...], row_1[:, W:], row_2[:, W:], from_l, from_r)
    copy.wait()


def sweep1_kernel(
    pos, arrived, volt, cleak, near, coef, u_o, src_o, cdiag, scale, c1, c2, r1, r2, r_s, c_s, v_s
):
    for o in range(NO):
        h = arrived[8 * o + 5 : 8 * o + 6, :].astype(jnp.int32)
        r_s[:, lanes(o)] = onehot(h >> 7, CB)
        c_s[:, lanes(o)] = onehot(h & (CB - 1), CB)
    diag = 4.0 * coarse_conductance + cleak[...] + via_conductance * nt(r_s[...], c_s[...])
    cdiag[...] = diag
    scale[...] = relaxation / diag
    tot = arrived[4:5, :]
    for o in range(1, NO):
        tot += arrived[8 * o + 4 : 8 * o + 5, :]
    d = solve(tot)
    sub = iota((8, L), 0)
    cf = jnp.zeros((8, L), F32)
    for k in range(4):
        cf = jnp.where(sub == k, d[k], cf)
    coef[...] = cf
    for o in range(NO):
        v = jnp.sum(arrived[8 * o : 8 * o + 8, :] * cf, axis=0, keepdims=True)
        hi, lo = hi_lo(v)
        on = c_s[:, lanes(o)]
        v_s[:, lanes(o)] = on * hi.astype(BF16)
        v_s[:, lanes(NO + o)] = on * lo.astype(BF16)
    src = nt(r_s[...], v_s[:, : NO * L]) + nt(r_s[...], v_s[:, NO * L :])
    u = sweep(volt[...], src, diag, near[...])
    u_o[...] = u
    src_o[...] = src
    g, gl = iota((8, CB), 0), iota((8, CB), 1)
    to_l = nt(jnp.where(gl == g * GROUP, 1.0, 0.0), u, HI)
    to_r = nt(jnp.where(gl == g * GROUP + GROUP - 1, 1.0, 0.0), u, HI)
    c1[...], c2[...] = pair_order(pos, 1, to_l, to_r)
    r1[...], r2[...] = pair_order(pos, 0, u[0:8, :], u[CB - 8 :, :])


def sweep2_kernel(pos, u, src, cdiag, scale, col_1, col_2, row_1, row_2, u_o):
    from_l, from_r = from_pairs(pos, 1, col_1[...], col_2[...])
    near = coarse_neighbours(pos, u[...], row_1[...], row_2[...], from_l, from_r)
    u_o[...] = u[...] + scale[...] * (src[...] - (cdiag[...] * u[...] - coarse_conductance * near))


VM = pl.BlockSpec(memory_space=pltpu.VMEM)
ANY = pl.BlockSpec(memory_space=pltpu.HBM)
vmem = pltpu.MemorySpace.VMEM
hbm = jax.ShapeDtypeStruct


def keep(*args):
    return [pltpu.with_memory_space_constraint(x, pltpu.VMEM) for x in args]


def leave(*args):
    return [pltpu.with_memory_space_constraint(x, pltpu.HBM) for x in args]


def call(body, outs, args, scratch=(), flops=0, any_in=0, any_out=0):
    specs = [ANY] * any_in + [VM] * (len(args) - any_in)
    return pl.pallas_call(
        body,
        out_shape=outs,
        in_specs=specs,
        out_specs=[ANY] * any_out + [VM] * (len(outs) - any_out),
        scratch_shapes=list(scratch),
        cost_estimate=pl.CostEstimate(flops=flops, bytes_accessed=0, transcendentals=0),
        compiler_params=pltpu.CompilerParams(vmem_limit_bytes=20 * 2**20),
    )(*args)


def pairs(axis, other, ring):
    n, m = lax.axis_size(axis), lax.axis_size(other)
    near = [(i, i ^ 1) for i in range(n)]
    far = []
    for i in range(n):
        for k in range(m):
            to = (((i + 1) ^ 1) - 1 & (n - 1), k)
            if not ring and i in (0, n - 1):
                to = (i, k ^ 1)
            ids = [(p, q) if axis == ROW else (q, p) for p, q in ((i, k), to)]
            far.append(tuple(r * lax.axis_size(COL) + c for r, c in ids))
    return near, sorted(far)


def exchange(axis, first, second, ring=False):
    near, far = pairs(axis, COL if axis == ROW else ROW, ring)
    if ring:
        n = lax.axis_size(axis)
        far = [(i, ((i + 1) ^ 1) - 1 & (n - 1)) for i in range(n)]
        return lax.ppermute(first, axis, near), lax.ppermute(second, axis, far)
    return lax.ppermute(first, axis, near), lax.ppermute(second, (ROW, COL), far)


def spread(x, axis=COL):
    return lax.all_to_all(x, axis, split_axis=0, concat_axis=0, tiled=True)


def per_device(load_amp, load_mask, leak, coarse_leak, coarse_init, via_fine, via_coarse, via_count):
    pos = jnp.where(
        lax.broadcasted_iota(jnp.int32, (8, W + CB), 0) == 0, lax.axis_index(ROW), lax.axis_index(COL)
    ).astype(jnp.int32)
    live = jnp.arange(L, dtype=jnp.int32)[None, :] < via_count.reshape(NO, 1)
    wt = jnp.where(live, via_conductance, 0.0).astype(F32)
    fine = via_fine.reshape(NO, L)
    coarse = via_coarse.reshape(NO, L)
    tile, block, slots = vmem((T, T), F32), vmem((CB, CB), F32), vmem((NO, L), F32)
    hot, chot = vmem((T, NO * L), BF16), vmem((CB, NO * L), BF16)
    hots = vmem((T, 2 * NO * L), BF16)
    rim16, side, seam = vmem((16, T), F32), vmem((8, T), F32), vmem((8, CB), F32)
    ext, packed = vmem((LT + 1, EXT, L), F32), ((L, L), F32)
    dmas = pltpu.SemaphoreType.DMA((4,))
    big = 20_000_000_000

    blocks = call(
        copies_kernel, [pltpu.MemorySpace.HBM((NO * CB, CB), F32)], leave(coarse_init),
        [pltpu.SemaphoreType.DMA((NO,))], any_out=1,
    )[0]
    blocks = spread(blocks)
    node, where, fine, via = call(
        parts_kernel,
        [slots, pltpu.MemorySpace.HBM((2 * NO, L), jnp.int32),
         vmem((NO, L), jnp.int32), pltpu.MemorySpace.HBM((T, T), F32)],
        leave(fine, coarse) + keep(wt), [hot, hot], flops=big,
    )
    zl, invd, strips, irims = call(
        diag_kernel, [tile, tile, rim16, rim16],
        leave(load_amp, load_mask, leak, via),
        [tile, vmem((T, T), jnp.int32), tile, tile, dmas], flops=big, any_in=4,
    )
    a, send_1, send_2, injected = call(
        strips_kernel, [hot, side, side, slots],
        keep(pos, blocks, node, fine, wt, strips),
    )
    col_1, col_2 = exchange(COL, send_1, send_2)
    z, zrims = call(
        rhs_kernel, [tile, rim16], keep(fine, injected, zl, invd, a), [hots], flops=big
    )
    rim = vmem((8, W + CB), F32)
    send_1, send_2, corners = call(
        edge_kernel, [rim, rim, vmem((64, L), F32)],
        keep(pos, zrims, irims, col_1, col_2, coarse_init)    )
    row_1, row_2 = exchange(ROW, send_1, send_2)
    hist, acc = call(
        basis_kernel, [pltpu.MemorySpace.HBM((4, LT, T, L), F32), vmem((8 * SUMS, L), F32)], keep(pos, z, invd, col_1, col_2),
        [ext] * 5 + [dmas], flops=big, any_out=1,
    )
    rims, part = call(
        rim_kernel, [vmem((48, T), F32), vmem((8, L), F32)],
        keep(pos, z, invd, corners, row_1, row_2, acc)    )
    rows = spread(part, ROW)
    g = call(
        gather_kernel, [vmem(*packed)], leave(hist, where) + keep(rims, wt),
        [vmem((4, LT, T, L), F32), vmem((T * SLAB + 8, L), F32),
         pltpu.MemorySpace.SMEM((2 * NO, L), jnp.int32), pltpu.SemaphoreType.DMA((5,))],
        flops=big, any_in=2,
    )[0]
    arrived = spread(call(pack_kernel, [vmem(*packed)], keep(g, rows, node))[0])
    near, ahead = call(
        base_kernel, [block, vmem((AHEAD, LT, T, L), F32)],
        leave(hist, blocks) + keep(pos, coarse_init, row_1, row_2),
        [vmem((NO * CB, CB), F32), dmas], flops=big, any_in=2,
    )
    coef, u, src, cdiag, scale, c1, c2, r1, r2 = call(
        sweep1_kernel, [seam, block, block, block, block, seam, seam, seam, seam],
        keep(pos, arrived, coarse_init, coarse_leak, near),
        [chot, chot, vmem((CB, 2 * NO * L), BF16)],
    )
    c1, c2 = exchange(COL, c1, c2, ring=True)
    r1, r2 = exchange(ROW, r1, r2)
    fine_drop = call(
        combine_kernel, [pltpu.MemorySpace.HBM((T, T), F32)], leave(hist) + keep(ahead, coef, rims),
        [vmem((STEPS, 4 - AHEAD, LT, T // STEPS, L), F32), tile, pltpu.SemaphoreType.DMA((STEPS,)),
         pltpu.SemaphoreType.DMA((STEPS,))], flops=big // 4, any_in=1, any_out=1,
    )[0]
    coarse_drop = call(
        sweep2_kernel, [hbm((CB, CB), F32)], keep(pos, u, src, cdiag, scale, c1, c2, r1, r2)    )[0]
    return fine_drop, coarse_drop


def solution(mesh):
    spec = P(ROW, COL)

    return jax.shard_map(
        per_device, mesh=mesh, in_specs=(spec,) * 8, out_specs=(spec, spec), check_vma=False
    )
```

profile of v0, /device:TPU:1, one launch (start us, length us, event | category | flops | bytes accessed | tf_op | source)
XLA Modules:
  0.0 75.0 jit_solution(6590929995048363197)
XLA Ops:
  0.6 2.0 %shard_map.96 = f32[2048,128]{1,0:T(8,128)} custom-call(f32[128,128]{1,0:T(8,128)} %volt.7), custom_call_target="tpu_custom_call" | custom-call | tf_op jit(solution)/shard_map/pallas_call | solution.py:568
  2.6 7.6 %all-to-all-start = ((f32[16,128,128]{2,1,0:T(8,128)}), f32[16,128,128]{2,1,0:T(8,128)S(1)}, u32[]{:S(2)}, u32[]{:S(2)}) async-start(f32[16,128,128]{2,1,0:T(8,128)} %bitcast.15), calls=%async_computation | async-start | bytes 2097152 | tf_op jit(solution)/shard_map/all_to_all | solution.py:603
  10.2 0.7 fusion.wt
  10.9 3.5 %shard_map.95 = (f32[16,128]{1,0:T(8,128)S(1)}, s32[32,128]{1,0:T(8,128)}, s32[16,128]{1,0:T(8,128)S(1)}, f32[512,512]{1,0:T(8,128)}) custom-call(s32[16,128]{1,0:T(8,128)} %bitcast.17, s32[16,128]{1,0:T(8,128)} %bitcast.18, f32[16,128]{1,0:T(8,128)S(1)} %fusion.wt), custom_call_target="tpu_custom_call" | custom-call | flops 20000000000 | tf_op jit(solution)/shard_map/pallas_call | solution.py:568
  14.4 3.1 %shard_map.97 = (f32[512,512]{1,0:T(8,128)S(1)}, f32[512,512]{1,0:T(8,128)S(1)}, f32[16,512]{1,0:T(8,128)S(1)}, f32[16,512]{1,0:T(8,128)S(1)}) custom-call(f32[512,512]{1,0:T(8,128)} %amp.1, s32[512,512]{1,0:T(8,128)} %mask.1, f32[512,512]{1,0:T(8,128)} %leak.1, f32[512,512]{1,0:T(8,128)} %get-tuple-element.36.via), custom_call_target="tpu_custom_call" | custom-call | flops 20000000000 | tf_op jit(solution)/shard_map/pallas_call | solution.py:568
  17.5 8.7 %all-to-all-done = f32[16,128,128]{2,1,0:T(8,128)S(1)} async-done(((f32[16,128,128]{2,1,0:T(8,128)}), f32[16,128,128]{2,1,0:T(8,128)S(1)}, u32[]{:S(2)}, u32[]{:S(2)}) %all-to-all-start) | async-done | bytes 1048608 | tf_op jit(solution)/shard_map/all_to_all | solution.py:603
  26.3 1.6 %shard_map.98 = (bf16[512,2048]{1,0:T(8,128)(2,1)S(1)}, f32[8,512]{1,0:T(8,128)S(1)}, f32[8,512]{1,0:T(8,128)S(1)}, f32[16,128]{1,0:T(8,128)S(1)}) custom-call(s32[8,768]{1,0:T(8,128)S(1)} %iota.11.pos, f32[2048,128]{1,0:T(8,128)S(1)} %bitcast.11, f32[16,128]{1,0:T(8,128)S(1)} %get-tuple-element.35.node, s32[16,128]{1,0:T(8,128)S(1)} %get-tuple-element.34.vf, ...), custom_call_target="tpu_custom_call" | custom-call | tf_op jit(solution)/shard_map/pallas_call | solution.py:568
  28.2 2.4 %collective-permute-start.1 = (f32[8,512]{1,0:T(8,128)S(1)}, f32[8,512]{1,0:T(8,128)S(1)}, u32[]{:S(2)}, u32[]{:S(2)}) collective-permute-start(f32[8,512]{1,0:T(8,128)S(1)} %get-tuple-element.44), channel_id=1, source_target_pairs={{0,16},{1,2},{2,1},{3,4},{4,3},{5,6},{6,5},{7,8},{8,7},{9,10},{10,... | collective-permute-start | bytes 49160 | tf_op jit(solution)/shard_map/ppermute | solution.py:599
  30.6 2.8 %shard_map.99 = (f32[512,512]{1,0:T(8,128)S(1)}, f32[16,512]{1,0:T(8,128)S(1)}) custom-call(s32[16,128]{1,0:T(8,128)S(1)} %get-tuple-element.34.vf, f32[16,128]{1,0:T(8,128)S(1)} %get-tuple-element.38.injected, f32[512,512]{1,0:T(8,128)S(1)} %get-tuple-element.39.zl, f32[512,512]{1,0:T(8,128)S(1)} %get-tuple-element.40.invd, ...), custom_call_target="tpu_custom_call" | custom-call | flops 20000000000 | tf_op jit(solution)/shard_map/pallas_call | solution.py:568
  33.7 0.9 %collective-permute-start.2 = (f32[8,768]{1,0:T(8,128)S(1)}, f32[8,768]{1,0:T(8,128)S(1)}, u32[]{:S(2)}, u32[]{:S(2)}) collective-permute-start(f32[8,768]{1,0:T(8,128)S(1)} %get-tuple-element.48), channel_id=1, source_target_pairs={{0,16},{16,0},{32,48},{48,32},{64,80},{80,64},{96,112},{112,96},{1... | collective-permute-start | bytes 73736 | tf_op jit(solution)/shard_map/ppermute | solution.py:599
  34.6 1.6 %collective-permute-start.3 = (f32[8,768]{1,0:T(8,128)S(1)}, f32[8,768]{1,0:T(8,128)S(1)}, u32[]{:S(2)}, u32[]{:S(2)}) collective-permute-start(f32[8,768]{1,0:T(8,128)S(1)} %get-tuple-element.49), channel_id=1, source_target_pairs={{0,1},{1,0},{2,3},{3,2},{4,5},{5,4},{6,7},{7,6},{8,9},{9,8},{10,11... | collective-permute-start | bytes 73736 | tf_op jit(solution)/shard_map/ppermute | solution.py:599
  36.2 4.8 %shard_map.100 = (f32[4,4,512,128]{3,2,1,0:T(8,128)}, f32[64,128]{1,0:T(8,128)S(1)}) custom-call(s32[8,768]{1,0:T(8,128)S(1)} %iota.11.pos, f32[512,512]{1,0:T(8,128)S(1)} %get-tuple-element.42.z, f32[512,512]{1,0:T(8,128)S(1)} %get-tuple-element.40.invd, f32[8,512]{1,0:T(8,128)S(1)} %collective-permute-done.col_1, f32[8,512]{1,0:T(8,128)S(1)} %collective-permute-done.1.col_2), custom_call_target="tpu_custom_call" | custom-call | flops 20000000000 | tf_op jit(solution)/shard_map/pallas_call | solution.py:568
  41.0 1.2 %shard_map.103 = (f32[48,512]{1,0:T(8,128)S(1)}, f32[8,128]{1,0:T(8,128)}) custom-call(s32[8,768]{1,0:T(8,128)S(1)} %iota.11.pos, f32[512,512]{1,0:T(8,128)S(1)} %get-tuple-element.42.z, f32[512,512]{1,0:T(8,128)S(1)} %get-tuple-element.40.invd, f32[64,128]{1,0:T(8,128)S(1)} %get-tuple-element.52.corners, f32[8,768]{1,0:T(8,128)S(1)} %collective-permute-done.2.row_1, ...), custom_call_target="tpu_custom_call" | custom-call | tf_op jit(solution)/shard_map/pallas_call | solution.py:568
  42.2 5.5 %all-to-all-start.1 = ((f32[8,1,128]{2,1,0:T(1,128)}), f32[8,1,128]{2,1,0:T(1,128)S(1)}, u32[]{:S(2)}, u32[]{:S(2)}) async-start(f32[8,1,128]{2,1,0:T(1,128)} %bitcast.6), calls=%async_computation.1 | async-start | bytes 8192 | tf_op jit(solution)/shard_map/all_to_all | solution.py:603
  47.7 4.6 %shard_map.104.g = f32[128,128]{1,0:T(8,128)S(1)} custom-call(f32[4,4,512,128]{3,2,1,0:T(8,128)} %get-tuple-element.45.hist, s32[32,128]{1,0:T(8,128)} %get-tuple-element.51.table, f32[48,512]{1,0:T(8,128)S(1)} %get-tuple-element.54.rims, f32[16,128]{1,0:T(8,128)S(1)} %fusion.wt), custom_call_target="tpu_custom_call" | custom-call | flops 20000000000 | tf_op jit(solution)/shard_map/pallas_call | solution.py:568
  53.0 4.6 %all-to-all-start.2 = ((f32[16,8,128]{2,1,0:T(8,128)}), f32[16,8,128]{2,1,0:T(8,128)S(1)}, u32[]{:S(2)}, u32[]{:S(2)}) async-start(f32[16,8,128]{2,1,0:T(8,128)} %bitcast.8), calls=%async_computation.2 | async-start | bytes 131072 | tf_op jit(solution)/shard_map/all_to_all | solution.py:603
  57.6 2.0 %shard_map.102 = (f32[128,128]{1,0:T(8,128)S(1)}, f32[1,4,512,128]{3,2,1,0:T(8,128)S(1)}) custom-call(f32[4,4,512,128]{3,2,1,0:T(8,128)} %get-tuple-element.45.hist, f32[2048,128]{1,0:T(8,128)} %bitcast.12, s32[8,768]{1,0:T(8,128)S(1)} %iota.11.pos, f32[128,128]{1,0:T(8,128)S(1)} %copy-done.1, f32[8,768]{1,0:T(8,128)S(1)} %collective-permute-done.2.row_1, ...), custom_call_target="tpu_custom_call" | custom-call | flops 20000000000 | tf_op jit(solution)/shard_map/pallas_call | solution.py:568
  59.6 4.5 %all-to-all-done.2 = f32[16,8,128]{2,1,0:T(8,128)S(1)} async-done(((f32[16,8,128]{2,1,0:T(8,128)}), f32[16,8,128]{2,1,0:T(8,128)S(1)}, u32[]{:S(2)}, u32[]{:S(2)}) %all-to-all-start.2) | async-done | bytes 65568 | tf_op jit(solution)/shard_map/all_to_all | solution.py:603
  64.1 1.6 %shard_map.106 = (f32[8,128]{1,0:T(8,128)S(1)}, f32[128,128]{1,0:T(8,128)S(1)}, f32[128,128]{1,0:T(8,128)S(1)}, f32[128,128]{1,0:T(8,128)S(1)}, f32[128,128]{1,0...) custom-call(s32[8,768]{1,0:T(8,128)S(1)} %iota.11.pos, ...), custom_call_target="tpu_custom_call" | custom-call | tf_op jit(solution)/shard_map/pallas_call | solution.py:568
  66.0 1.6 %collective-permute-start.5 = (f32[8,128]{1,0:T(8,128)S(1)}, f32[8,128]{1,0:T(8,128)S(1)}, u32[]{:S(2)}, u32[]{:S(2)}) collective-permute-start(f32[8,128]{1,0:T(8,128)S(1)} %get-tuple-element.63), channel_id=1, source_target_pairs={{0,15},{1,2},{2,1},{3,4},{4,3},{5,6},{6,5},{7,8},{8,7},{9,10},{10,... | collective-permute-start | bytes 12296 | tf_op jit(solution)/shard_map/ppermute | solution.py:598
  67.6 2.7 %collective-permute-start.6 = (f32[8,128]{1,0:T(8,128)S(1)}, f32[8,128]{1,0:T(8,128)S(1)}, u32[]{:S(2)}, u32[]{:S(2)}) collective-permute-start(f32[8,128]{1,0:T(8,128)S(1)} %get-tuple-element.64), channel_id=1, source_target_pairs={{0,16},{16,0},{32,48},{48,32},{64,80},{80,64},{96,112},{112,96},{1... | collective-permute-start | bytes 12296 | tf_op jit(solution)/shard_map/ppermute | solution.py:599
  70.3 1.0 %collective-permute-start.7 = (f32[8,128]{1,0:T(8,128)S(1)}, f32[8,128]{1,0:T(8,128)S(1)}, u32[]{:S(2)}, u32[]{:S(2)}) collective-permute-start(f32[8,128]{1,0:T(8,128)S(1)} %get-tuple-element.65), channel_id=1, source_target_pairs={{0,1},{1,0},{2,3},{3,2},{4,5},{5,4},{6,7},{7,6},{8,9},{9,8},{10,11... | collective-permute-start | bytes 12296 | tf_op jit(solution)/shard_map/ppermute | solution.py:599
  71.3 2.7 %shard_map.107 = f32[512,512]{1,0:T(8,128)} custom-call(f32[4,4,512,128]{3,2,1,0:T(8,128)} %get-tuple-element.45.hist, f32[1,4,512,128]{3,2,1,0:T(8,128)S(1)} %get-tuple-element.50.ahead, f32[8,128]{1,0:T(8,128)S(1)} %get-tuple-element.57.coef, f32[48,512]{1,0:T(8,128)S(1)} %get-tuple-element.54.rims), custom_call_target="tpu_custom_call" | custom-call | flops 5000000000 | tf_op jit(solution)/shard_map/pallas_call | solution.py:568
  74.0 1.0 %shard_map.108 = f32[128,128]{1,0:T(8,128)} custom-call(s32[8,768]{1,0:T(8,128)S(1)} %iota.11.pos, f32[128,128]{1,0:T(8,128)S(1)} %get-tuple-element.58.u, f32[128,128]{1,0:T(8,128)S(1)} %get-tuple-element.59.src, f32[128,128]{1,0:T(8,128)S(1)} %get-tuple-element.60.cdiag, f32[128,128]{1,0:T(8,128)S(1)} %get-tuple-element.61.scale, ...), custom_call_target="tpu_custom_call" | custom-call | tf_op jit(solution)/shard_map/pallas_call | solution.py:568
  (21 shorter events, 1.6 us)
Async XLA Ops:
  2.6 23.6 %all-to-all-start = ((f32[16,128,128]{2,1,0:T(8,128)}), f32[16,128,128]{2,1,0:T(8,128)S(1)}, u32[]{:S(2)}, u32[]{:S(2)}) async-start(f32[16,128,128]{2,1,0:T(8,128)} %bitcast.15), calls=%async_computation | async-start | bytes 2097152 | tf_op jit(solution)/shard_map/all_to_all | solution.py:603
  26.3 7.2 %copy-start = (f32[16,128,128]{2,1,0:T(8,128)}, f32[16,128,128]{2,1,0:T(8,128)S(1)}, u32[]{:S(2)}) copy-start(f32[16,128,128]{2,1,0:T(8,128)S(1)} %all-to-all-done) | copy-start | bytes 3145732
  27.9 5.5 %collective-permute-start = (f32[8,512]{1,0:T(8,128)S(1)}, f32[8,512]{1,0:T(8,128)S(1)}, u32[]{:S(2)}, u32[]{:S(2)}) collective-permute-start(f32[8,512]{1,0:T(8,128)S(1)} %get-tuple-element.43), channel_id=1, source_target_pairs={{0,1},{1,0},{2,3},{3,2},{4,5},{5,4},{6,7},{7,6},{8,9},{9,8},{10,11... | collective-permute-start | bytes 49160 | tf_op jit(solution)/shard_map/ppermute | solution.py:599
  28.2 5.2 %collective-permute-start.1 = (f32[8,512]{1,0:T(8,128)S(1)}, f32[8,512]{1,0:T(8,128)S(1)}, u32[]{:S(2)}, u32[]{:S(2)}) collective-permute-start(f32[8,512]{1,0:T(8,128)S(1)} %get-tuple-element.44), channel_id=1, source_target_pairs={{0,16},{1,2},{2,1},{3,4},{4,3},{5,6},{6,5},{7,8},{8,7},{9,10},{10,... | collective-permute-start | bytes 49160 | tf_op jit(solution)/shard_map/ppermute | solution.py:599
  30.6 2.8 %copy-start.1 = (f32[128,128]{1,0:T(8,128)S(1)}, f32[128,128]{1,0:T(8,128)}, u32[]{:S(2)}) copy-start(f32[128,128]{1,0:T(8,128)} %volt.7) | copy-start | bytes 196612
  33.7 7.3 %collective-permute-start.2 = (f32[8,768]{1,0:T(8,128)S(1)}, f32[8,768]{1,0:T(8,128)S(1)}, u32[]{:S(2)}, u32[]{:S(2)}) collective-permute-start(f32[8,768]{1,0:T(8,128)S(1)} %get-tuple-element.48), channel_id=1, source_target_pairs={{0,16},{16,0},{32,48},{48,32},{64,80},{80,64},{96,112},{112,96},{1... | collective-permute-start | bytes 73736 | tf_op jit(solution)/shard_map/ppermute | solution.py:599
  34.6 6.4 %collective-permute-start.3 = (f32[8,768]{1,0:T(8,128)S(1)}, f32[8,768]{1,0:T(8,128)S(1)}, u32[]{:S(2)}, u32[]{:S(2)}) collective-permute-start(f32[8,768]{1,0:T(8,128)S(1)} %get-tuple-element.49), channel_id=1, source_target_pairs={{0,1},{1,0},{2,3},{3,2},{4,5},{5,4},{6,7},{7,6},{8,9},{9,8},{10,11... | collective-permute-start | bytes 73736 | tf_op jit(solution)/shard_map/ppermute | solution.py:599
  42.2 10.2 %all-to-all-start.1 = ((f32[8,1,128]{2,1,0:T(1,128)}), f32[8,1,128]{2,1,0:T(1,128)S(1)}, u32[]{:S(2)}, u32[]{:S(2)}) async-start(f32[8,1,128]{2,1,0:T(1,128)} %bitcast.6), calls=%async_computation.1 | async-start | bytes 8192 | tf_op jit(solution)/shard_map/all_to_all | solution.py:603
  53.0 11.2 %all-to-all-start.2 = ((f32[16,8,128]{2,1,0:T(8,128)}), f32[16,8,128]{2,1,0:T(8,128)S(1)}, u32[]{:S(2)}, u32[]{:S(2)}) async-start(f32[16,8,128]{2,1,0:T(8,128)} %bitcast.8), calls=%async_computation.2 | async-start | bytes 131072 | tf_op jit(solution)/shard_map/all_to_all | solution.py:603
  57.6 6.5 %copy-start.2 = (f32[128,128]{1,0:T(8,128)S(1)}, f32[128,128]{1,0:T(8,128)}, u32[]{:S(2)}) copy-start(f32[128,128]{1,0:T(8,128)} %cleak.1) | copy-start | bytes 196612
  65.7 8.2 %collective-permute-start.4 = (f32[8,128]{1,0:T(8,128)S(1)}, f32[8,128]{1,0:T(8,128)S(1)}, u32[]{:S(2)}, u32[]{:S(2)}) collective-permute-start(f32[8,128]{1,0:T(8,128)S(1)} %get-tuple-element.62), channel_id=1, source_target_pairs={{0,1},{1,0},{2,3},{3,2},{4,5},{5,4},{6,7},{7,6},{8,9},{9,8},{10,11... | collective-permute-start | bytes 12296 | tf_op jit(solution)/shard_map/ppermute | solution.py:598
  66.0 7.9 %collective-permute-start.5 = (f32[8,128]{1,0:T(8,128)S(1)}, f32[8,128]{1,0:T(8,128)S(1)}, u32[]{:S(2)}, u32[]{:S(2)}) collective-permute-start(f32[8,128]{1,0:T(8,128)S(1)} %get-tuple-element.63), channel_id=1, source_target_pairs={{0,15},{1,2},{2,1},{3,4},{4,3},{5,6},{6,5},{7,8},{8,7},{9,10},{10,... | collective-permute-start | bytes 12296 | tf_op jit(solution)/shard_map/ppermute | solution.py:598
  67.6 6.3 %collective-permute-start.6 = (f32[8,128]{1,0:T(8,128)S(1)}, f32[8,128]{1,0:T(8,128)S(1)}, u32[]{:S(2)}, u32[]{:S(2)}) collective-permute-start(f32[8,128]{1,0:T(8,128)S(1)} %get-tuple-element.64), channel_id=1, source_target_pairs={{0,16},{16,0},{32,48},{48,32},{64,80},{80,64},{96,112},{112,96},{1... | collective-permute-start | bytes 12296 | tf_op jit(solution)/shard_map/ppermute | solution.py:599
  70.3 3.7 %collective-permute-start.7 = (f32[8,128]{1,0:T(8,128)S(1)}, f32[8,128]{1,0:T(8,128)S(1)}, u32[]{:S(2)}, u32[]{:S(2)}) collective-permute-start(f32[8,128]{1,0:T(8,128)S(1)} %get-tuple-element.65), channel_id=1, source_target_pairs={{0,1},{1,0},{2,3},{3,2},{4,5},{5,4},{6,7},{7,6},{8,9},{9,8},{10,11... | collective-permute-start | bytes 12296 | tf_op jit(solution)/shard_map/ppermute | solution.py:599
where the time goes:
time: 75.4 us; the launch traced here: 75 us
  Pallas kernels  31.5 us (42%)
  starting transfers between devices  28.6 us (38%)
  waiting for transfers between devices  13.3 us (18%)
  between operations  0.83 us (1%)
    pallas_call x14, Pallas kernels, call(): pl.pallas_call(body, out_shape=outs, in_specs=specs, out_specs=[ANY] * an...  31.5 us
    all_to_all x3, starting transfers between devices, spread(): return lax.all_to_all(x, axis, split_axis=0, concat_axis=0, tiled=True)  17.8 us
    all_to_all x3, waiting for transfers between devices, spread(): return lax.all_to_all(x, axis, split_axis=0, concat_axis=0, tiled=True)  13.2 us
    ppermute x3, starting transfers between devices, exchange(): lax.ppermute(second, (ROW, COL), far)  4.97 us
    ppermute x3, starting transfers between devices, exchange(): lax.ppermute(first, axis, near)  3.91 us
    ppermute x2, starting transfers between devices, exchange(): return (lax.ppermute(first, axis, near), lax.ppermute(second, axis, far))  1.94 us
  transfers between devices with their start and end apart: 11, of which 2 were waited for; matrix products, arithmetic and copies ran while one was open for 1% of the time, Pallas kernels for 31%

commit v1 on v0

--- a/solution.py
+++ b/solution.py
@@ -292,27 +292,41 @@
         copy.wait()
 
 
-def gram_terms(acc):
+def gram_terms(acc, powers):
     g0, q0 = acc[0], acc[1]
     m = acc[2:]
     r = [q0, q0 - m[0], q0 - m[0] - m[1]]
-    h = {(0, 0): q0, **{(0, j): RHO[0] * m[j - 1] for j in (1, 2, 3)}}
-    b = [g0] + r
+    b0, h00 = g0, q0
     for k in range(3):
-        h[0, 0] = h[0, 0] - Q[k] * m[k]
-        b[0] = b[0] - Q[k] * r[k]
+        h00 = h00 - Q[k] * m[k]
+        b0 = b0 - Q[k] * r[k]
     for k in range(6):
         f = sum(Q[j] * RHO[k - j] for j in range(3) if 0 <= k - j < 4)
-        h[0, 0] = h[0, 0] - f * m[k]
-    for j in (1, 2, 3):
-        for k in (1, 2, 3):
-            h[0, j] = h[0, j] + RHO[k] * m[j - 1 + k]
-            if j <= k:
-                h[j, k] = m[j + k - 2] - m[j + k - 1]
-    out = []
-    for p in range(4):
-        out += [h[p, q] for q in range(p, 4)] + [b[p]]
+        h00 = h00 - f * m[k]
+
+    def times(p, q):
+        out = [0.0] * (len(p) + len(q) - 1)
+        for i, x in enumerate(p):
+            for j, y in enumerate(q):
+                out[i + j] += x * y
+        return out
+
+    def total(p, values):
+        out = None
+        for x, v in zip(p, values):
+            if x != 0.0:
+                out = x * v if out is None else out + x * v
+        return out
+
+    out = [h00] + [total(times(RHO, p), m) for p in powers] + [b0]
+    for i in range(3):
+        out += [total(times(times(powers[i], powers[k]), (1.0, -1.0)), m) for k in range(i, 3)]
+        out.append(total(powers[i], r))
     return out
+
+
+PLAIN = ((1.0,), (0.0, 1.0), (0.0, 0.0, 1.0))
+SHIFTED = ((1.0,), (1.0, 1.0), (1.0, 2.0, 1.0))
 
 
 def rim_kernel(pos, z, invd, corners, row_1, row_2, acc_i, rims, part):
@@ -343,16 +357,17 @@
             acc[k] = acc[k] + fold(p)
         for k, x in enumerate((wo, n1o, n2o)):
             rims[16 * k + 8 * end : 16 * k + 8 * end + 8, :] = x
-    terms = gram_terms(acc)
-    rows14 = jnp.concatenate(
-        [jnp.sum(a, axis=0, keepdims=True) for a in terms] + [jnp.zeros((2, L), F32)], axis=0
-    )
-    a, rest = hi_lo(rows14)
+    two = [jnp.zeros((2, L), F32)]
+    rows = []
+    for powers in (PLAIN, SHIFTED):
+        terms = gram_terms(acc, powers)
+        rows += [jnp.sum(a, axis=0, keepdims=True) for a in terms] + two
+    a, rest = hi_lo(jnp.concatenate(rows, axis=0))
     b, c = hi_lo(rest)
     parts = jnp.concatenate([c, b, a], axis=0).astype(BF16)
     sums = nt(jnp.ones((8, L), BF16), parts)
-    sums = sums[:, 0:16] + sums[:, 16:32] + sums[:, 32:48]
-    sums = jnp.concatenate([sums, jnp.zeros((8, L - 16), F32)], axis=1)
+    sums = sums[:, 0:32] + sums[:, 32:64] + sums[:, 64:96]
+    sums = jnp.concatenate([sums, jnp.zeros((8, L - 32), F32)], axis=1)
     part[...] = sums
 
 
@@ -399,8 +414,11 @@
 def solve(tot):
     lane = iota((1, L), 1)
 
+    def lane_of(x, k):
+        return jnp.sum(jnp.where(lane == k, x, 0.0), axis=1, keepdims=True)
+
     def pick(k):
-        return jnp.sum(jnp.where(lane == k, tot, 0.0), axis=1, keepdims=True)
+        return jnp.where(lane == 0, lane_of(tot, k), lane_of(tot, 16 + k))
 
     h, b = {}, []
     k = 0
@@ -410,10 +428,11 @@
             k += 1
         b.append(pick(k))
         k += 1
-    floor = [3e-7 * h[p, p] for p in range(4)]
-    inv = []
+    size = [h[p, p] for p in range(4)]
+    inv, worst = [], jnp.ones((1, L), F32)
     for p in range(4):
-        inv.append(jnp.where(h[p, p] > floor[p], 1.0 / h[p, p], 0.0))
+        inv.append(jnp.where(h[p, p] > 3e-7 * size[p], 1.0 / h[p, p], 0.0))
+        worst = jnp.minimum(worst, jnp.where(size[p] > 0.0, h[p, p] / size[p], 0.0))
         for q in range(p + 1, 4):
             f = h[p, q] * inv[p]
             for r in range(q, 4):
@@ -425,6 +444,11 @@
         for q in range(p + 1, 4):
             s = s - h[p, q] * c[q]
         c[p] = s * inv[p]
+    shifted = lane_of(worst, 1) > lane_of(worst, 0)
+    plain = [lane_of(x, 0) for x in c]
+    other = [lane_of(x, 1) for x in c]
+    other[1:] = [other[1] + other[2] + other[3], other[2] + 2.0 * other[3], other[3]]
+    c = [jnp.where(shifted, y, x) for x, y in zip(plain, other)]
     return [c[0]] + [c[k + 1] - Q[k] * c[0] for k in range(3)]
 
 

time: 75.4 us -> 75.5 us (level)
  no operation moved by 1% of the time
where the time goes in v1:
time: 75.5 us; the launch traced here: 75 us
  Pallas kernels  31.6 us (42%)
  starting transfers between devices  28.6 us (38%)
  waiting for transfers between devices  13.3 us (18%)
  between operations  0.83 us (1%)
    pallas_call x14, Pallas kernels, call(): pl.pallas_call(body, out_shape=outs, in_specs=specs, out_specs=[ANY] * an...  31.6 us
    all_to_all x3, starting transfers between devices, spread(): return lax.all_to_all(x, axis, split_axis=0, concat_axis=0, tiled=True)  17.8 us
    all_to_all x3, waiting for transfers between devices, spread(): return lax.all_to_all(x, axis, split_axis=0, concat_axis=0, tiled=True)  13.2 us
    ppermute x3, starting transfers between devices, exchange(): lax.ppermute(second, (ROW, COL), far)  4.97 us
    ppermute x3, starting transfers between devices, exchange(): lax.ppermute(first, axis, near)  3.91 us
    ppermute x2, starting transfers between devices, exchange(): return (lax.ppermute(first, axis, near), lax.ppermute(second, axis, far))  1.94 us
  transfers between devices with their start and end apart: 11, of which 2 were waited for; matrix products, arithmetic and copies ran while one was open for 1% of the time, Pallas kernels for 31%

profile of v1, /device:TPU:1, one launch (start us, length us, event | category | flops | bytes accessed | tf_op | source)
XLA Modules:
  0.0 75.0 jit_solution(4487743466687513531)
XLA Ops:
  0.6 2.0 %shard_map.96 = f32[2048,128]{1,0:T(8,128)} custom-call(f32[128,128]{1,0:T(8,128)} %volt.7), custom_call_target="tpu_custom_call" | custom-call | tf_op jit(solution)/shard_map/pallas_call | solution.py:592
  2.6 7.6 %all-to-all-start = ((f32[16,128,128]{2,1,0:T(8,128)}), f32[16,128,128]{2,1,0:T(8,128)S(1)}, u32[]{:S(2)}, u32[]{:S(2)}) async-start(f32[16,128,128]{2,1,0:T(8,128)} %bitcast.15), calls=%async_computation | async-start | bytes 2097152 | tf_op jit(solution)/shard_map/all_to_all | solution.py:627
  10.2 0.7 fusion.wt
  10.9 3.5 %shard_map.95 = (f32[16,128]{1,0:T(8,128)S(1)}, s32[32,128]{1,0:T(8,128)}, s32[16,128]{1,0:T(8,128)S(1)}, f32[512,512]{1,0:T(8,128)}) custom-call(s32[16,128]{1,0:T(8,128)} %bitcast.17, s32[16,128]{1,0:T(8,128)} %bitcast.18, f32[16,128]{1,0:T(8,128)S(1)} %fusion.wt), custom_call_target="tpu_custom_call" | custom-call | flops 20000000000 | tf_op jit(solution)/shard_map/pallas_call | solution.py:592
  14.4 3.1 %shard_map.97 = (f32[512,512]{1,0:T(8,128)S(1)}, f32[512,512]{1,0:T(8,128)S(1)}, f32[16,512]{1,0:T(8,128)S(1)}, f32[16,512]{1,0:T(8,128)S(1)}) custom-call(f32[512,512]{1,0:T(8,128)} %amp.1, s32[512,512]{1,0:T(8,128)} %mask.1, f32[512,512]{1,0:T(8,128)} %leak.1, f32[512,512]{1,0:T(8,128)} %get-tuple-element.36.via), custom_call_target="tpu_custom_call" | custom-call | flops 20000000000 | tf_op jit(solution)/shard_map/pallas_call | solution.py:592
  17.5 8.7 %all-to-all-done = f32[16,128,128]{2,1,0:T(8,128)S(1)} async-done(((f32[16,128,128]{2,1,0:T(8,128)}), f32[16,128,128]{2,1,0:T(8,128)S(1)}, u32[]{:S(2)}, u32[]{:S(2)}) %all-to-all-start) | async-done | bytes 1048608 | tf_op jit(solution)/shard_map/all_to_all | solution.py:627
  26.3 1.6 %shard_map.98 = (bf16[512,2048]{1,0:T(8,128)(2,1)S(1)}, f32[8,512]{1,0:T(8,128)S(1)}, f32[8,512]{1,0:T(8,128)S(1)}, f32[16,128]{1,0:T(8,128)S(1)}) custom-call(s32[8,768]{1,0:T(8,128)S(1)} %iota.11.pos, f32[2048,128]{1,0:T(8,128)S(1)} %bitcast.11, f32[16,128]{1,0:T(8,128)S(1)} %get-tuple-element.35.node, s32[16,128]{1,0:T(8,128)S(1)} %get-tuple-element.34.vf, ...), custom_call_target="tpu_custom_call" | custom-call | tf_op jit(solution)/shard_map/pallas_call | solution.py:592
  28.2 2.4 %collective-permute-start.1 = (f32[8,512]{1,0:T(8,128)S(1)}, f32[8,512]{1,0:T(8,128)S(1)}, u32[]{:S(2)}, u32[]{:S(2)}) collective-permute-start(f32[8,512]{1,0:T(8,128)S(1)} %get-tuple-element.44), channel_id=1, source_target_pairs={{0,16},{1,2},{2,1},{3,4},{4,3},{5,6},{6,5},{7,8},{8,7},{9,10},{10,... | collective-permute-start | bytes 49160 | tf_op jit(solution)/shard_map/ppermute | solution.py:623
  30.6 2.8 %shard_map.99 = (f32[512,512]{1,0:T(8,128)S(1)}, f32[16,512]{1,0:T(8,128)S(1)}) custom-call(s32[16,128]{1,0:T(8,128)S(1)} %get-tuple-element.34.vf, f32[16,128]{1,0:T(8,128)S(1)} %get-tuple-element.38.injected, f32[512,512]{1,0:T(8,128)S(1)} %get-tuple-element.39.zl, f32[512,512]{1,0:T(8,128)S(1)} %get-tuple-element.40.invd, ...), custom_call_target="tpu_custom_call" | custom-call | flops 20000000000 | tf_op jit(solution)/shard_map/pallas_call | solution.py:592
  33.7 0.9 %collective-permute-start.2 = (f32[8,768]{1,0:T(8,128)S(1)}, f32[8,768]{1,0:T(8,128)S(1)}, u32[]{:S(2)}, u32[]{:S(2)}) collective-permute-start(f32[8,768]{1,0:T(8,128)S(1)} %get-tuple-element.48), channel_id=1, source_target_pairs={{0,16},{16,0},{32,48},{48,32},{64,80},{80,64},{96,112},{112,96},{1... | collective-permute-start | bytes 73736 | tf_op jit(solution)/shard_map/ppermute | solution.py:623
  34.6 1.6 %collective-permute-start.3 = (f32[8,768]{1,0:T(8,128)S(1)}, f32[8,768]{1,0:T(8,128)S(1)}, u32[]{:S(2)}, u32[]{:S(2)}) collective-permute-start(f32[8,768]{1,0:T(8,128)S(1)} %get-tuple-element.49), channel_id=1, source_target_pairs={{0,1},{1,0},{2,3},{3,2},{4,5},{5,4},{6,7},{7,6},{8,9},{9,8},{10,11... | collective-permute-start | bytes 73736 | tf_op jit(solution)/shard_map/ppermute | solution.py:623
  36.2 4.8 %shard_map.100 = (f32[4,4,512,128]{3,2,1,0:T(8,128)}, f32[64,128]{1,0:T(8,128)S(1)}) custom-call(s32[8,768]{1,0:T(8,128)S(1)} %iota.11.pos, f32[512,512]{1,0:T(8,128)S(1)} %get-tuple-element.42.z, f32[512,512]{1,0:T(8,128)S(1)} %get-tuple-element.40.invd, f32[8,512]{1,0:T(8,128)S(1)} %collective-permute-done.col_1, f32[8,512]{1,0:T(8,128)S(1)} %collective-permute-done.1.col_2), custom_call_target="tpu_custom_call" | custom-call | flops 20000000000 | tf_op jit(solution)/shard_map/pallas_call | solution.py:592
  41.0 1.2 %shard_map.103 = (f32[48,512]{1,0:T(8,128)S(1)}, f32[8,128]{1,0:T(8,128)}) custom-call(s32[8,768]{1,0:T(8,128)S(1)} %iota.11.pos, f32[512,512]{1,0:T(8,128)S(1)} %get-tuple-element.42.z, f32[512,512]{1,0:T(8,128)S(1)} %get-tuple-element.40.invd, f32[64,128]{1,0:T(8,128)S(1)} %get-tuple-element.52.corners, f32[8,768]{1,0:T(8,128)S(1)} %collective-permute-done.2.row_1, ...), custom_call_target="tpu_custom_call" | custom-call | tf_op jit(solution)/shard_map/pallas_call | solution.py:592
  42.2 5.5 %all-to-all-start.1 = ((f32[8,1,128]{2,1,0:T(1,128)}), f32[8,1,128]{2,1,0:T(1,128)S(1)}, u32[]{:S(2)}, u32[]{:S(2)}) async-start(f32[8,1,128]{2,1,0:T(1,128)} %bitcast.6), calls=%async_computation.1 | async-start | bytes 8192 | tf_op jit(solution)/shard_map/all_to_all | solution.py:627
  47.7 4.6 %shard_map.104.g = f32[128,128]{1,0:T(8,128)S(1)} custom-call(f32[4,4,512,128]{3,2,1,0:T(8,128)} %get-tuple-element.45.hist, s32[32,128]{1,0:T(8,128)} %get-tuple-element.51.table, f32[48,512]{1,0:T(8,128)S(1)} %get-tuple-element.54.rims, f32[16,128]{1,0:T(8,128)S(1)} %fusion.wt), custom_call_target="tpu_custom_call" | custom-call | flops 20000000000 | tf_op jit(solution)/shard_map/pallas_call | solution.py:592
  53.0 4.6 %all-to-all-start.2 = ((f32[16,8,128]{2,1,0:T(8,128)}), f32[16,8,128]{2,1,0:T(8,128)S(1)}, u32[]{:S(2)}, u32[]{:S(2)}) async-start(f32[16,8,128]{2,1,0:T(8,128)} %bitcast.8), calls=%async_computation.2 | async-start | bytes 131072 | tf_op jit(solution)/shard_map/all_to_all | solution.py:627
  57.6 2.0 %shard_map.102 = (f32[128,128]{1,0:T(8,128)S(1)}, f32[1,4,512,128]{3,2,1,0:T(8,128)S(1)}) custom-call(f32[4,4,512,128]{3,2,1,0:T(8,128)} %get-tuple-element.45.hist, f32[2048,128]{1,0:T(8,128)} %bitcast.12, s32[8,768]{1,0:T(8,128)S(1)} %iota.11.pos, f32[128,128]{1,0:T(8,128)S(1)} %copy-done.1, f32[8,768]{1,0:T(8,128)S(1)} %collective-permute-done.2.row_1, ...), custom_call_target="tpu_custom_call" | custom-call | flops 20000000000 | tf_op jit(solution)/shard_map/pallas_call | solution.py:592
  59.7 4.5 %all-to-all-done.2 = f32[16,8,128]{2,1,0:T(8,128)S(1)} async-done(((f32[16,8,128]{2,1,0:T(8,128)}), f32[16,8,128]{2,1,0:T(8,128)S(1)}, u32[]{:S(2)}, u32[]{:S(2)}) %all-to-all-start.2) | async-done | bytes 65568 | tf_op jit(solution)/shard_map/all_to_all | solution.py:627
  64.1 1.6 %shard_map.106 = (f32[8,128]{1,0:T(8,128)S(1)}, f32[128,128]{1,0:T(8,128)S(1)}, f32[128,128]{1,0:T(8,128)S(1)}, f32[128,128]{1,0:T(8,128)S(1)}, f32[128,128]{1,0...) custom-call(s32[8,768]{1,0:T(8,128)S(1)} %iota.11.pos, ...), custom_call_target="tpu_custom_call" | custom-call | tf_op jit(solution)/shard_map/pallas_call | solution.py:592
  66.1 1.6 %collective-permute-start.5 = (f32[8,128]{1,0:T(8,128)S(1)}, f32[8,128]{1,0:T(8,128)S(1)}, u32[]{:S(2)}, u32[]{:S(2)}) collective-permute-start(f32[8,128]{1,0:T(8,128)S(1)} %get-tuple-element.63), channel_id=1, source_target_pairs={{0,15},{1,2},{2,1},{3,4},{4,3},{5,6},{6,5},{7,8},{8,7},{9,10},{10,... | collective-permute-start | bytes 12296 | tf_op jit(solution)/shard_map/ppermute | solution.py:622
  67.7 2.7 %collective-permute-start.6 = (f32[8,128]{1,0:T(8,128)S(1)}, f32[8,128]{1,0:T(8,128)S(1)}, u32[]{:S(2)}, u32[]{:S(2)}) collective-permute-start(f32[8,128]{1,0:T(8,128)S(1)} %get-tuple-element.64), channel_id=1, source_target_pairs={{0,16},{16,0},{32,48},{48,32},{64,80},{80,64},{96,112},{112,96},{1... | collective-permute-start | bytes 12296 | tf_op jit(solution)/shard_map/ppermute | solution.py:623
  70.4 1.0 %collective-permute-start.7 = (f32[8,128]{1,0:T(8,128)S(1)}, f32[8,128]{1,0:T(8,128)S(1)}, u32[]{:S(2)}, u32[]{:S(2)}) collective-permute-start(f32[8,128]{1,0:T(8,128)S(1)} %get-tuple-element.65), channel_id=1, source_target_pairs={{0,1},{1,0},{2,3},{3,2},{4,5},{5,4},{6,7},{7,6},{8,9},{9,8},{10,11... | collective-permute-start | bytes 12296 | tf_op jit(solution)/shard_map/ppermute | solution.py:623
  71.3 2.7 %shard_map.107 = f32[512,512]{1,0:T(8,128)} custom-call(f32[4,4,512,128]{3,2,1,0:T(8,128)} %get-tuple-element.45.hist, f32[1,4,512,128]{3,2,1,0:T(8,128)S(1)} %get-tuple-element.50.ahead, f32[8,128]{1,0:T(8,128)S(1)} %get-tuple-element.57.coef, f32[48,512]{1,0:T(8,128)S(1)} %get-tuple-element.54.rims), custom_call_target="tpu_custom_call" | custom-call | flops 5000000000 | tf_op jit(solution)/shard_map/pallas_call | solution.py:592
  74.0 1.0 %shard_map.108 = f32[128,128]{1,0:T(8,128)} custom-call(s32[8,768]{1,0:T(8,128)S(1)} %iota.11.pos, f32[128,128]{1,0:T(8,128)S(1)} %get-tuple-element.58.u, f32[128,128]{1,0:T(8,128)S(1)} %get-tuple-element.59.src, f32[128,128]{1,0:T(8,128)S(1)} %get-tuple-element.60.cdiag, f32[128,128]{1,0:T(8,128)S(1)} %get-tuple-element.61.scale, ...), custom_call_target="tpu_custom_call" | custom-call | tf_op jit(solution)/shard_map/pallas_call | solution.py:592
  (21 shorter events, 1.6 us)
Async XLA Ops:
  2.6 23.6 %all-to-all-start = ((f32[16,128,128]{2,1,0:T(8,128)}), f32[16,128,128]{2,1,0:T(8,128)S(1)}, u32[]{:S(2)}, u32[]{:S(2)}) async-start(f32[16,128,128]{2,1,0:T(8,128)} %bitcast.15), calls=%async_computation | async-start | bytes 2097152 | tf_op jit(solution)/shard_map/all_to_all | solution.py:627
  26.3 7.2 %copy-start = (f32[16,128,128]{2,1,0:T(8,128)}, f32[16,128,128]{2,1,0:T(8,128)S(1)}, u32[]{:S(2)}) copy-start(f32[16,128,128]{2,1,0:T(8,128)S(1)} %all-to-all-done) | copy-start | bytes 3145732
  27.9 5.5 %collective-permute-start = (f32[8,512]{1,0:T(8,128)S(1)}, f32[8,512]{1,0:T(8,128)S(1)}, u32[]{:S(2)}, u32[]{:S(2)}) collective-permute-start(f32[8,512]{1,0:T(8,128)S(1)} %get-tuple-element.43), channel_id=1, source_target_pairs={{0,1},{1,0},{2,3},{3,2},{4,5},{5,4},{6,7},{7,6},{8,9},{9,8},{10,11... | collective-permute-start | bytes 49160 | tf_op jit(solution)/shard_map/ppermute | solution.py:623
  28.2 5.2 %collective-permute-start.1 = (f32[8,512]{1,0:T(8,128)S(1)}, f32[8,512]{1,0:T(8,128)S(1)}, u32[]{:S(2)}, u32[]{:S(2)}) collective-permute-start(f32[8,512]{1,0:T(8,128)S(1)} %get-tuple-element.44), channel_id=1, source_target_pairs={{0,16},{1,2},{2,1},{3,4},{4,3},{5,6},{6,5},{7,8},{8,7},{9,10},{10,... | collective-permute-start | bytes 49160 | tf_op jit(solution)/shard_map/ppermute | solution.py:623
  30.6 2.8 %copy-start.1 = (f32[128,128]{1,0:T(8,128)S(1)}, f32[128,128]{1,0:T(8,128)}, u32[]{:S(2)}) copy-start(f32[128,128]{1,0:T(8,128)} %volt.7) | copy-start | bytes 196612
  33.7 7.3 %collective-permute-start.2 = (f32[8,768]{1,0:T(8,128)S(1)}, f32[8,768]{1,0:T(8,128)S(1)}, u32[]{:S(2)}, u32[]{:S(2)}) collective-permute-start(f32[8,768]{1,0:T(8,128)S(1)} %get-tuple-element.48), channel_id=1, source_target_pairs={{0,16},{16,0},{32,48},{48,32},{64,80},{80,64},{96,112},{112,96},{1... | collective-permute-start | bytes 73736 | tf_op jit(solution)/shard_map/ppermute | solution.py:623
  34.6 6.4 %collective-permute-start.3 = (f32[8,768]{1,0:T(8,128)S(1)}, f32[8,768]{1,0:T(8,128)S(1)}, u32[]{:S(2)}, u32[]{:S(2)}) collective-permute-start(f32[8,768]{1,0:T(8,128)S(1)} %get-tuple-element.49), channel_id=1, source_target_pairs={{0,1},{1,0},{2,3},{3,2},{4,5},{5,4},{6,7},{7,6},{8,9},{9,8},{10,11... | collective-permute-start | bytes 73736 | tf_op jit(solution)/shard_map/ppermute | solution.py:623
  42.2 10.2 %all-to-all-start.1 = ((f32[8,1,128]{2,1,0:T(1,128)}), f32[8,1,128]{2,1,0:T(1,128)S(1)}, u32[]{:S(2)}, u32[]{:S(2)}) async-start(f32[8,1,128]{2,1,0:T(1,128)} %bitcast.6), calls=%async_computation.1 | async-start | bytes 8192 | tf_op jit(solution)/shard_map/all_to_all | solution.py:627
  53.0 11.2 %all-to-all-start.2 = ((f32[16,8,128]{2,1,0:T(8,128)}), f32[16,8,128]{2,1,0:T(8,128)S(1)}, u32[]{:S(2)}, u32[]{:S(2)}) async-start(f32[16,8,128]{2,1,0:T(8,128)} %bitcast.8), calls=%async_computation.2 | async-start | bytes 131072 | tf_op jit(solution)/shard_map/all_to_all | solution.py:627
  57.6 6.5 %copy-start.2 = (f32[128,128]{1,0:T(8,128)S(1)}, f32[128,128]{1,0:T(8,128)}, u32[]{:S(2)}) copy-start(f32[128,128]{1,0:T(8,128)} %cleak.1) | copy-start | bytes 196612
  65.8 8.2 %collective-permute-start.4 = (f32[8,128]{1,0:T(8,128)S(1)}, f32[8,128]{1,0:T(8,128)S(1)}, u32[]{:S(2)}, u32[]{:S(2)}) collective-permute-start(f32[8,128]{1,0:T(8,128)S(1)} %get-tuple-element.62), channel_id=1, source_target_pairs={{0,1},{1,0},{2,3},{3,2},{4,5},{5,4},{6,7},{7,6},{8,9},{9,8},{10,11... | collective-permute-start | bytes 12296 | tf_op jit(solution)/shard_map/ppermute | solution.py:622
  66.1 7.9 %collective-permute-start.5 = (f32[8,128]{1,0:T(8,128)S(1)}, f32[8,128]{1,0:T(8,128)S(1)}, u32[]{:S(2)}, u32[]{:S(2)}) collective-permute-start(f32[8,128]{1,0:T(8,128)S(1)} %get-tuple-element.63), channel_id=1, source_target_pairs={{0,15},{1,2},{2,1},{3,4},{4,3},{5,6},{6,5},{7,8},{8,7},{9,10},{10,... | collective-permute-start | bytes 12296 | tf_op jit(solution)/shard_map/ppermute | solution.py:622
  67.7 6.3 %collective-permute-start.6 = (f32[8,128]{1,0:T(8,128)S(1)}, f32[8,128]{1,0:T(8,128)S(1)}, u32[]{:S(2)}, u32[]{:S(2)}) collective-permute-start(f32[8,128]{1,0:T(8,128)S(1)} %get-tuple-element.64), channel_id=1, source_target_pairs={{0,16},{16,0},{32,48},{48,32},{64,80},{80,64},{96,112},{112,96},{1... | collective-permute-start | bytes 12296 | tf_op jit(solution)/shard_map/ppermute | solution.py:623
  70.4 3.7 %collective-permute-start.7 = (f32[8,128]{1,0:T(8,128)S(1)}, f32[8,128]{1,0:T(8,128)S(1)}, u32[]{:S(2)}, u32[]{:S(2)}) collective-permute-start(f32[8,128]{1,0:T(8,128)S(1)} %get-tuple-element.65), channel_id=1, source_target_pairs={{0,1},{1,0},{2,3},{3,2},{4,5},{5,4},{6,7},{7,6},{8,9},{9,8},{10,11... | collective-permute-start | bytes 12296 | tf_op jit(solution)/shard_map/ppermute | solution.py:623

commit v2 on v1

--- a/solution.py
+++ b/solution.py
@@ -105,14 +105,9 @@
     rims[8:16, :] = inv[T - 8 :]
 
 
-def copies_kernel(volt, out, sem):
-    copies = [
-        pltpu.make_async_copy(volt, out.at[pl.ds(o * CB, CB), :], sem.at[o]) for o in range(NO)
-    ]
-    for copy in copies:
-        copy.start()
-    for copy in copies:
-        copy.wait()
+def copies_kernel(volt, out):
+    for o in range(NO):
+        out[o * CB : (o + 1) * CB, :] = volt[...]
 
 
 def parts_kernel(vf, vc, wt, node, slots, vf_o, via, a_s, b_s):
@@ -645,7 +640,6 @@
 
     blocks = call(
         copies_kernel, [pltpu.MemorySpace.HBM((NO * CB, CB), F32)], leave(coarse_init),
-        [pltpu.SemaphoreType.DMA((NO,))], any_out=1,
     )[0]
     blocks = spread(blocks)
     node, where, fine, via = call(

time: 75.5 us -> 75.4 us (level)
  no operation moved by 1% of the time
where the time goes in v2:
time: 75.4 us; the launch traced here: 74.9 us
  Pallas kernels  31.5 us (42%)
  starting transfers between devices  28.6 us (38%)
  waiting for transfers between devices  13.3 us (18%)
  between operations  0.82 us (1%)
    pallas_call x14, Pallas kernels, call(): pl.pallas_call(body, out_shape=outs, in_specs=specs, out_specs=[ANY] * an...  31.5 us
    all_to_all x3, starting transfers between devices, spread(): return lax.all_to_all(x, axis, split_axis=0, concat_axis=0, tiled=True)  17.8 us
    all_to_all x3, waiting for transfers between devices, spread(): return lax.all_to_all(x, axis, split_axis=0, concat_axis=0, tiled=True)  13.2 us
    ppermute x3, starting transfers between devices, exchange(): lax.ppermute(second, (ROW, COL), far)  4.97 us
    ppermute x3, starting transfers between devices, exchange(): lax.ppermute(first, axis, near)  3.91 us
    ppermute x2, starting transfers between devices, exchange(): return (lax.ppermute(first, axis, near), lax.ppermute(second, axis, far))  1.94 us
  transfers between devices with their start and end apart: 11, of which 2 were waited for; matrix products, arithmetic and copies ran while one was open for 1% of the time, Pallas kernels for 31%

profile of v2, /device:TPU:1, one launch (start us, length us, event | category | flops | bytes accessed | tf_op | source)
XLA Modules:
  0.0 74.9 jit_solution(15995642255219087923)
XLA Ops:
  0.6 1.9 %shard_map.96 = f32[2048,128]{1,0:T(8,128)} custom-call(f32[128,128]{1,0:T(8,128)} %volt.7), custom_call_target="tpu_custom_call" | custom-call | tf_op jit(solution)/shard_map/pallas_call | solution.py:587
  2.5 7.6 %all-to-all-start = ((f32[16,128,128]{2,1,0:T(8,128)}), f32[16,128,128]{2,1,0:T(8,128)S(1)}, u32[]{:S(2)}, u32[]{:S(2)}) async-start(f32[16,128,128]{2,1,0:T(8,128)} %bitcast.15), calls=%async_computation | async-start | bytes 2097152 | tf_op jit(solution)/shard_map/all_to_all | solution.py:622
  10.1 0.7 fusion.wt
  10.9 3.5 %shard_map.95 = (f32[16,128]{1,0:T(8,128)S(1)}, s32[32,128]{1,0:T(8,128)}, s32[16,128]{1,0:T(8,128)S(1)}, f32[512,512]{1,0:T(8,128)}) custom-call(s32[16,128]{1,0:T(8,128)} %bitcast.17, s32[16,128]{1,0:T(8,128)} %bitcast.18, f32[16,128]{1,0:T(8,128)S(1)} %fusion.wt), custom_call_target="tpu_custom_call" | custom-call | flops 20000000000 | tf_op jit(solution)/shard_map/pallas_call | solution.py:587
  14.3 3.1 %shard_map.97 = (f32[512,512]{1,0:T(8,128)S(1)}, f32[512,512]{1,0:T(8,128)S(1)}, f32[16,512]{1,0:T(8,128)S(1)}, f32[16,512]{1,0:T(8,128)S(1)}) custom-call(f32[512,512]{1,0:T(8,128)} %amp.1, s32[512,512]{1,0:T(8,128)} %mask.1, f32[512,512]{1,0:T(8,128)} %leak.1, f32[512,512]{1,0:T(8,128)} %get-tuple-element.36.via), custom_call_target="tpu_custom_call" | custom-call | flops 20000000000 | tf_op jit(solution)/shard_map/pallas_call | solution.py:587
  17.4 8.7 %all-to-all-done = f32[16,128,128]{2,1,0:T(8,128)S(1)} async-done(((f32[16,128,128]{2,1,0:T(8,128)}), f32[16,128,128]{2,1,0:T(8,128)S(1)}, u32[]{:S(2)}, u32[]{:S(2)}) %all-to-all-start) | async-done | bytes 1048608 | tf_op jit(solution)/shard_map/all_to_all | solution.py:622
  26.2 1.6 %shard_map.98 = (bf16[512,2048]{1,0:T(8,128)(2,1)S(1)}, f32[8,512]{1,0:T(8,128)S(1)}, f32[8,512]{1,0:T(8,128)S(1)}, f32[16,128]{1,0:T(8,128)S(1)}) custom-call(s32[8,768]{1,0:T(8,128)S(1)} %iota.11.pos, f32[2048,128]{1,0:T(8,128)S(1)} %bitcast.11, f32[16,128]{1,0:T(8,128)S(1)} %get-tuple-element.35.node, s32[16,128]{1,0:T(8,128)S(1)} %get-tuple-element.34.vf, ...), custom_call_target="tpu_custom_call" | custom-call | tf_op jit(solution)/shard_map/pallas_call | solution.py:587
  28.2 2.4 %collective-permute-start.1 = (f32[8,512]{1,0:T(8,128)S(1)}, f32[8,512]{1,0:T(8,128)S(1)}, u32[]{:S(2)}, u32[]{:S(2)}) collective-permute-start(f32[8,512]{1,0:T(8,128)S(1)} %get-tuple-element.44), channel_id=1, source_target_pairs={{0,16},{1,2},{2,1},{3,4},{4,3},{5,6},{6,5},{7,8},{8,7},{9,10},{10,... | collective-permute-start | bytes 49160 | tf_op jit(solution)/shard_map/ppermute | solution.py:618
  30.5 2.8 %shard_map.99 = (f32[512,512]{1,0:T(8,128)S(1)}, f32[16,512]{1,0:T(8,128)S(1)}) custom-call(s32[16,128]{1,0:T(8,128)S(1)} %get-tuple-element.34.vf, f32[16,128]{1,0:T(8,128)S(1)} %get-tuple-element.38.injected, f32[512,512]{1,0:T(8,128)S(1)} %get-tuple-element.39.zl, f32[512,512]{1,0:T(8,128)S(1)} %get-tuple-element.40.invd, ...), custom_call_target="tpu_custom_call" | custom-call | flops 20000000000 | tf_op jit(solution)/shard_map/pallas_call | solution.py:587
  33.6 0.9 %collective-permute-start.2 = (f32[8,768]{1,0:T(8,128)S(1)}, f32[8,768]{1,0:T(8,128)S(1)}, u32[]{:S(2)}, u32[]{:S(2)}) collective-permute-start(f32[8,768]{1,0:T(8,128)S(1)} %get-tuple-element.48), channel_id=1, source_target_pairs={{0,16},{16,0},{32,48},{48,32},{64,80},{80,64},{96,112},{112,96},{1... | collective-permute-start | bytes 73736 | tf_op jit(solution)/shard_map/ppermute | solution.py:618
  34.5 1.6 %collective-permute-start.3 = (f32[8,768]{1,0:T(8,128)S(1)}, f32[8,768]{1,0:T(8,128)S(1)}, u32[]{:S(2)}, u32[]{:S(2)}) collective-permute-start(f32[8,768]{1,0:T(8,128)S(1)} %get-tuple-element.49), channel_id=1, source_target_pairs={{0,1},{1,0},{2,3},{3,2},{4,5},{5,4},{6,7},{7,6},{8,9},{9,8},{10,11... | collective-permute-start | bytes 73736 | tf_op jit(solution)/shard_map/ppermute | solution.py:618
  36.1 4.8 %shard_map.100 = (f32[4,4,512,128]{3,2,1,0:T(8,128)}, f32[64,128]{1,0:T(8,128)S(1)}) custom-call(s32[8,768]{1,0:T(8,128)S(1)} %iota.11.pos, f32[512,512]{1,0:T(8,128)S(1)} %get-tuple-element.42.z, f32[512,512]{1,0:T(8,128)S(1)} %get-tuple-element.40.invd, f32[8,512]{1,0:T(8,128)S(1)} %collective-permute-done.col_1, f32[8,512]{1,0:T(8,128)S(1)} %collective-permute-done.1.col_2), custom_call_target="tpu_custom_call" | custom-call | flops 20000000000 | tf_op jit(solution)/shard_map/pallas_call | solution.py:587
  40.9 1.2 %shard_map.103 = (f32[48,512]{1,0:T(8,128)S(1)}, f32[8,128]{1,0:T(8,128)}) custom-call(s32[8,768]{1,0:T(8,128)S(1)} %iota.11.pos, f32[512,512]{1,0:T(8,128)S(1)} %get-tuple-element.42.z, f32[512,512]{1,0:T(8,128)S(1)} %get-tuple-element.40.invd, f32[64,128]{1,0:T(8,128)S(1)} %get-tuple-element.52.corners, f32[8,768]{1,0:T(8,128)S(1)} %collective-permute-done.2.row_1, ...), custom_call_target="tpu_custom_call" | custom-call | tf_op jit(solution)/shard_map/pallas_call | solution.py:587
  42.1 5.5 %all-to-all-start.1 = ((f32[8,1,128]{2,1,0:T(1,128)}), f32[8,1,128]{2,1,0:T(1,128)S(1)}, u32[]{:S(2)}, u32[]{:S(2)}) async-start(f32[8,1,128]{2,1,0:T(1,128)} %bitcast.6), calls=%async_computation.1 | async-start | bytes 8192 | tf_op jit(solution)/shard_map/all_to_all | solution.py:622
  47.6 4.6 %shard_map.104.g = f32[128,128]{1,0:T(8,128)S(1)} custom-call(f32[4,4,512,128]{3,2,1,0:T(8,128)} %get-tuple-element.45.hist, s32[32,128]{1,0:T(8,128)} %get-tuple-element.51.table, f32[48,512]{1,0:T(8,128)S(1)} %get-tuple-element.54.rims, f32[16,128]{1,0:T(8,128)S(1)} %fusion.wt), custom_call_target="tpu_custom_call" | custom-call | flops 20000000000 | tf_op jit(solution)/shard_map/pallas_call | solution.py:587
  52.9 4.6 %all-to-all-start.2 = ((f32[16,8,128]{2,1,0:T(8,128)}), f32[16,8,128]{2,1,0:T(8,128)S(1)}, u32[]{:S(2)}, u32[]{:S(2)}) async-start(f32[16,8,128]{2,1,0:T(8,128)} %bitcast.8), calls=%async_computation.2 | async-start | bytes 131072 | tf_op jit(solution)/shard_map/all_to_all | solution.py:622
  57.5 2.0 %shard_map.102 = (f32[128,128]{1,0:T(8,128)S(1)}, f32[1,4,512,128]{3,2,1,0:T(8,128)S(1)}) custom-call(f32[4,4,512,128]{3,2,1,0:T(8,128)} %get-tuple-element.45.hist, f32[2048,128]{1,0:T(8,128)} %bitcast.12, s32[8,768]{1,0:T(8,128)S(1)} %iota.11.pos, f32[128,128]{1,0:T(8,128)S(1)} %copy-done.1, f32[8,768]{1,0:T(8,128)S(1)} %collective-permute-done.2.row_1, ...), custom_call_target="tpu_custom_call" | custom-call | flops 20000000000 | tf_op jit(solution)/shard_map/pallas_call | solution.py:587
  59.6 4.5 %all-to-all-done.2 = f32[16,8,128]{2,1,0:T(8,128)S(1)} async-done(((f32[16,8,128]{2,1,0:T(8,128)}), f32[16,8,128]{2,1,0:T(8,128)S(1)}, u32[]{:S(2)}, u32[]{:S(2)}) %all-to-all-start.2) | async-done | bytes 65568 | tf_op jit(solution)/shard_map/all_to_all | solution.py:622
  64.1 1.6 %shard_map.106 = (f32[8,128]{1,0:T(8,128)S(1)}, f32[128,128]{1,0:T(8,128)S(1)}, f32[128,128]{1,0:T(8,128)S(1)}, f32[128,128]{1,0:T(8,128)S(1)}, f32[128,128]{1,0...) custom-call(s32[8,768]{1,0:T(8,128)S(1)} %iota.11.pos, ...), custom_call_target="tpu_custom_call" | custom-call | tf_op jit(solution)/shard_map/pallas_call | solution.py:587
  66.0 1.6 %collective-permute-start.5 = (f32[8,128]{1,0:T(8,128)S(1)}, f32[8,128]{1,0:T(8,128)S(1)}, u32[]{:S(2)}, u32[]{:S(2)}) collective-permute-start(f32[8,128]{1,0:T(8,128)S(1)} %get-tuple-element.63), channel_id=1, source_target_pairs={{0,15},{1,2},{2,1},{3,4},{4,3},{5,6},{6,5},{7,8},{8,7},{9,10},{10,... | collective-permute-start | bytes 12296 | tf_op jit(solution)/shard_map/ppermute | solution.py:617
  67.6 2.7 %collective-permute-start.6 = (f32[8,128]{1,0:T(8,128)S(1)}, f32[8,128]{1,0:T(8,128)S(1)}, u32[]{:S(2)}, u32[]{:S(2)}) collective-permute-start(f32[8,128]{1,0:T(8,128)S(1)} %get-tuple-element.64), channel_id=1, source_target_pairs={{0,16},{16,0},{32,48},{48,32},{64,80},{80,64},{96,112},{112,96},{1... | collective-permute-start | bytes 12296 | tf_op jit(solution)/shard_map/ppermute | solution.py:618
  70.3 1.0 %collective-permute-start.7 = (f32[8,128]{1,0:T(8,128)S(1)}, f32[8,128]{1,0:T(8,128)S(1)}, u32[]{:S(2)}, u32[]{:S(2)}) collective-permute-start(f32[8,128]{1,0:T(8,128)S(1)} %get-tuple-element.65), channel_id=1, source_target_pairs={{0,1},{1,0},{2,3},{3,2},{4,5},{5,4},{6,7},{7,6},{8,9},{9,8},{10,11... | collective-permute-start | bytes 12296 | tf_op jit(solution)/shard_map/ppermute | solution.py:618
  71.2 2.7 %shard_map.107 = f32[512,512]{1,0:T(8,128)} custom-call(f32[4,4,512,128]{3,2,1,0:T(8,128)} %get-tuple-element.45.hist, f32[1,4,512,128]{3,2,1,0:T(8,128)S(1)} %get-tuple-element.50.ahead, f32[8,128]{1,0:T(8,128)S(1)} %get-tuple-element.57.coef, f32[48,512]{1,0:T(8,128)S(1)} %get-tuple-element.54.rims), custom_call_target="tpu_custom_call" | custom-call | flops 5000000000 | tf_op jit(solution)/shard_map/pallas_call | solution.py:587
  74.0 1.0 %shard_map.108 = f32[128,128]{1,0:T(8,128)} custom-call(s32[8,768]{1,0:T(8,128)S(1)} %iota.11.pos, f32[128,128]{1,0:T(8,128)S(1)} %get-tuple-element.58.u, f32[128,128]{1,0:T(8,128)S(1)} %get-tuple-element.59.src, f32[128,128]{1,0:T(8,128)S(1)} %get-tuple-element.60.cdiag, f32[128,128]{1,0:T(8,128)S(1)} %get-tuple-element.61.scale, ...), custom_call_target="tpu_custom_call" | custom-call | tf_op jit(solution)/shard_map/pallas_call | solution.py:587
  (21 shorter events, 1.6 us)
Async XLA Ops:
  2.5 23.6 %all-to-all-start = ((f32[16,128,128]{2,1,0:T(8,128)}), f32[16,128,128]{2,1,0:T(8,128)S(1)}, u32[]{:S(2)}, u32[]{:S(2)}) async-start(f32[16,128,128]{2,1,0:T(8,128)} %bitcast.15), calls=%async_computation | async-start | bytes 2097152 | tf_op jit(solution)/shard_map/all_to_all | solution.py:622
  26.2 7.2 %copy-start = (f32[16,128,128]{2,1,0:T(8,128)}, f32[16,128,128]{2,1,0:T(8,128)S(1)}, u32[]{:S(2)}) copy-start(f32[16,128,128]{2,1,0:T(8,128)S(1)} %all-to-all-done) | copy-start | bytes 3145732
  27.8 5.5 %collective-permute-start = (f32[8,512]{1,0:T(8,128)S(1)}, f32[8,512]{1,0:T(8,128)S(1)}, u32[]{:S(2)}, u32[]{:S(2)}) collective-permute-start(f32[8,512]{1,0:T(8,128)S(1)} %get-tuple-element.43), channel_id=1, source_target_pairs={{0,1},{1,0},{2,3},{3,2},{4,5},{5,4},{6,7},{7,6},{8,9},{9,8},{10,11... | collective-permute-start | bytes 49160 | tf_op jit(solution)/shard_map/ppermute | solution.py:618
  28.2 5.2 %collective-permute-start.1 = (f32[8,512]{1,0:T(8,128)S(1)}, f32[8,512]{1,0:T(8,128)S(1)}, u32[]{:S(2)}, u32[]{:S(2)}) collective-permute-start(f32[8,512]{1,0:T(8,128)S(1)} %get-tuple-element.44), channel_id=1, source_target_pairs={{0,16},{1,2},{2,1},{3,4},{4,3},{5,6},{6,5},{7,8},{8,7},{9,10},{10,... | collective-permute-start | bytes 49160 | tf_op jit(solution)/shard_map/ppermute | solution.py:618
  30.5 2.8 %copy-start.1 = (f32[128,128]{1,0:T(8,128)S(1)}, f32[128,128]{1,0:T(8,128)}, u32[]{:S(2)}) copy-start(f32[128,128]{1,0:T(8,128)} %volt.7) | copy-start | bytes 196612
  33.6 7.3 %collective-permute-start.2 = (f32[8,768]{1,0:T(8,128)S(1)}, f32[8,768]{1,0:T(8,128)S(1)}, u32[]{:S(2)}, u32[]{:S(2)}) collective-permute-start(f32[8,768]{1,0:T(8,128)S(1)} %get-tuple-element.48), channel_id=1, source_target_pairs={{0,16},{16,0},{32,48},{48,32},{64,80},{80,64},{96,112},{112,96},{1... | collective-permute-start | bytes 73736 | tf_op jit(solution)/shard_map/ppermute | solution.py:618
  34.5 6.4 %collective-permute-start.3 = (f32[8,768]{1,0:T(8,128)S(1)}, f32[8,768]{1,0:T(8,128)S(1)}, u32[]{:S(2)}, u32[]{:S(2)}) collective-permute-start(f32[8,768]{1,0:T(8,128)S(1)} %get-tuple-element.49), channel_id=1, source_target_pairs={{0,1},{1,0},{2,3},{3,2},{4,5},{5,4},{6,7},{7,6},{8,9},{9,8},{10,11... | collective-permute-start | bytes 73736 | tf_op jit(solution)/shard_map/ppermute | solution.py:618
  42.1 10.2 %all-to-all-start.1 = ((f32[8,1,128]{2,1,0:T(1,128)}), f32[8,1,128]{2,1,0:T(1,128)S(1)}, u32[]{:S(2)}, u32[]{:S(2)}) async-start(f32[8,1,128]{2,1,0:T(1,128)} %bitcast.6), calls=%async_computation.1 | async-start | bytes 8192 | tf_op jit(solution)/shard_map/all_to_all | solution.py:622
  52.9 11.2 %all-to-all-start.2 = ((f32[16,8,128]{2,1,0:T(8,128)}), f32[16,8,128]{2,1,0:T(8,128)S(1)}, u32[]{:S(2)}, u32[]{:S(2)}) async-start(f32[16,8,128]{2,1,0:T(8,128)} %bitcast.8), calls=%async_computation.2 | async-start | bytes 131072 | tf_op jit(solution)/shard_map/all_to_all | solution.py:622
  57.5 6.5 %copy-start.2 = (f32[128,128]{1,0:T(8,128)S(1)}, f32[128,128]{1,0:T(8,128)}, u32[]{:S(2)}) copy-start(f32[128,128]{1,0:T(8,128)} %cleak.1) | copy-start | bytes 196612
  65.7 8.2 %collective-permute-start.4 = (f32[8,128]{1,0:T(8,128)S(1)}, f32[8,128]{1,0:T(8,128)S(1)}, u32[]{:S(2)}, u32[]{:S(2)}) collective-permute-start(f32[8,128]{1,0:T(8,128)S(1)} %get-tuple-element.62), channel_id=1, source_target_pairs={{0,1},{1,0},{2,3},{3,2},{4,5},{5,4},{6,7},{7,6},{8,9},{9,8},{10,11... | collective-permute-start | bytes 12296 | tf_op jit(solution)/shard_map/ppermute | solution.py:617
  66.0 7.9 %collective-permute-start.5 = (f32[8,128]{1,0:T(8,128)S(1)}, f32[8,128]{1,0:T(8,128)S(1)}, u32[]{:S(2)}, u32[]{:S(2)}) collective-permute-start(f32[8,128]{1,0:T(8,128)S(1)} %get-tuple-element.63), channel_id=1, source_target_pairs={{0,15},{1,2},{2,1},{3,4},{4,3},{5,6},{6,5},{7,8},{8,7},{9,10},{10,... | collective-permute-start | bytes 12296 | tf_op jit(solution)/shard_map/ppermute | solution.py:617
  67.6 6.3 %collective-permute-start.6 = (f32[8,128]{1,0:T(8,128)S(1)}, f32[8,128]{1,0:T(8,128)S(1)}, u32[]{:S(2)}, u32[]{:S(2)}) collective-permute-start(f32[8,128]{1,0:T(8,128)S(1)} %get-tuple-element.64), channel_id=1, source_target_pairs={{0,16},{16,0},{32,48},{48,32},{64,80},{80,64},{96,112},{112,96},{1... | collective-permute-start | bytes 12296 | tf_op jit(solution)/shard_map/ppermute | solution.py:618
  70.3 3.7 %collective-permute-start.7 = (f32[8,128]{1,0:T(8,128)S(1)}, f32[8,128]{1,0:T(8,128)S(1)}, u32[]{:S(2)}, u32[]{:S(2)}) collective-permute-start(f32[8,128]{1,0:T(8,128)S(1)} %get-tuple-element.65), channel_id=1, source_target_pairs={{0,1},{1,0},{2,3},{3,2},{4,5},{5,4},{6,7},{7,6},{8,9},{9,8},{10,11... | collective-permute-start | bytes 12296 | tf_op jit(solution)/shard_map/ppermute | solution.py:618
